TPU v7x, 256 devices: a 8x8x2 block of a 8x8x16 slice. The times are simulated.
256 devices in a mesh: member: 2 (over z), graph: 64 (over y, x), chan: 2 (over core).
Axes of the slice: x: 8, y: 8, z: 2, core: 2. Of those that a mesh axis runs over, the one named last changes fastest.
The devices are a block of a 8x8x16 slice.
Arguments:
- grid_state: bfloat16 [131072, 256], P(('member', 'graph')), parts along dimension 0, may hold values from -6 to 6
- w_src: bfloat16 [256, 512], P(None, 'chan'), may hold values from -0.375 to 0.375
- bias_src: float32 [512], P('chan'), may hold values from -3 to 3
- mesh_embed: bfloat16 [40960, 512], P('graph', 'chan'), may hold values from -6 to 6
- w_node: bfloat16 [512, 512], P('chan'), may hold values from -0.25 to 0.25
- w_dec: bfloat16 [512, 256], P('chan'), may hold values from -0.125 to 0.125
- slot_src: int32 [64, 64, 128], P('graph'), may hold values from 0 to 1023, as said below
- slot_dst: int32 [64, 64, 128], P(None, 'graph'), may hold values from 0 to 639, as said below
- slot_count: int32 [64, 64], replicated, may hold values from 1 to 128, as said below
Outputs:
- grid_out: bfloat16 [131072, 256], P(('member', 'graph'), 'chan'), parts along dimension 0
There are 2 independent parts, one for each index of `member`. A program takes and returns all parts, laid end to end along the dimension named above; an argument that names none is the same for every part. Nothing has to cross between parts.
Inputs may be any that keep to these rules, and one draw needn't show every extreme that they name: `slot_src`: slots at or past the live count hold arbitrary values in the same range. `slot_dst`: slots at or past the live count hold arbitrary values in the same range. slot_count[s, d] counts the live leading slots of the 128 from shard s to shard d; in every draw some receiving shard has all 128 slots live from every sender.
All inputs are finite; a program needn't handle non-finite values.
Results may differ from a plain program's by a relative error of at most 0.0056.
Values may be sent and summed in bfloat16 or wider, within the bound.
A program may use at most 64 MiB of HBM per device.

v0:
```python
import math

import jax
import jax.numpy as jnp
from jax import lax
from jax.sharding import PartitionSpec as P


def split_up(value, dim, count):
    lengths = value.shape
    parts = value.reshape(*lengths[:dim], count, lengths[dim] // count, *lengths[dim + 1 :])
    return jnp.moveaxis(parts, dim, 0)


def sum_at_owner(value, axis, dim):
    parts = split_up(value, dim, lax.axis_size(axis))
    arrived = lax.all_to_all(parts, axis, split_axis=0, concat_axis=0, tiled=True)
    return arrived.sum(axis=0)


def edge_network(source_rows, w_src, bias_src):
    return jax.nn.silu(
        jnp.dot(source_rows, w_src, preferred_element_type=jnp.float32) + bias_src
    ).astype(jnp.bfloat16)


def segment_rows(values, indices, usable, row_count):
    slot_total = values.shape[0]
    width = values.shape[1]
    block_len = math.gcd(slot_total, 2048)
    block_count = slot_total // block_len
    targets = jnp.where(usable, indices, -1).reshape(block_count, block_len)
    pieces = values.reshape(block_count, block_len, width)
    row_ids = jnp.arange(row_count, dtype=jnp.int32)

    def add_block(summed, scan_item):
        row_target, piece_vals = scan_item
        one_hot = (row_ids[:, None] == row_target[None, :]).astype(jnp.bfloat16)
        return (summed + jnp.dot(one_hot, piece_vals, preferred_element_type=jnp.float32), None)

    result, unused = lax.scan(
        add_block, jnp.zeros((row_count, width), jnp.float32), (targets, pieces)
    )
    return result


def on_device(
    grid_state, w_src, bias_src, mesh_embed, w_node, w_dec, slot_src, slot_dst, slot_count
):
    peers = lax.axis_size("graph")
    own_index = lax.axis_index("graph")
    core_index = lax.axis_index("chan")
    capacity = slot_src.shape[2]
    positions = jnp.arange(capacity, dtype=jnp.int32)
    grid_rows = grid_state.shape[0]
    mesh_rows = mesh_embed.shape[0]
    sent_counts = lax.dynamic_slice_in_dim(slot_count, own_index, 1, 0)[0]
    recv_counts = lax.dynamic_slice_in_dim(slot_count, own_index, 1, 1)[:, 0]
    half_slots = capacity // 2
    chosen = lax.dynamic_slice_in_dim(slot_src[0], core_index * half_slots, half_slots, 1)
    picked = jnp.take(grid_state, chosen.reshape(-1), axis=0).reshape(
        peers, half_slots, grid_state.shape[1]
    )
    arrived = lax.all_to_all(picked, "graph", split_axis=0, concat_axis=0, tiled=True)
    joined = lax.all_gather(arrived, "chan", axis=1, tiled=True)
    messages = edge_network(joined.reshape(peers * capacity, grid_state.shape[1]), w_src, bias_src)
    arrive_ok = (positions[None, :] < recv_counts[:, None]).reshape(-1)
    dst_rows = slot_dst[:, 0, :].reshape(-1)
    aggregate = segment_rows(messages, dst_rows, arrive_ok, mesh_rows)
    partial_hidden = jnp.dot(
        aggregate.astype(jnp.bfloat16), w_node, preferred_element_type=jnp.float32
    )
    hidden_pre = sum_at_owner(partial_hidden, "chan", 1)
    latent = (mesh_embed.astype(jnp.float32) + jax.nn.silu(hidden_pre)).astype(jnp.bfloat16)
    partial_proj = jnp.dot(latent, w_dec, preferred_element_type=jnp.float32)
    projected = sum_at_owner(partial_proj, "chan", 1).astype(jnp.bfloat16)
    returned = jnp.take(projected, dst_rows, axis=0).reshape(peers, capacity, projected.shape[1])
    came_back = lax.all_to_all(returned, "graph", split_axis=0, concat_axis=0, tiled=True).reshape(
        peers * capacity, projected.shape[1]
    )
    send_ok = (positions[None, :] < sent_counts[:, None]).reshape(-1)
    decoded = segment_rows(came_back, slot_src[0].reshape(-1), send_ok, grid_rows)
    width_half = decoded.shape[1]
    own_cols = lax.dynamic_slice_in_dim(grid_state, core_index * width_half, width_half, 1)
    return (own_cols.astype(jnp.float32) + decoded).astype(jnp.bfloat16)


def solution(mesh):
    placed = (
        P(("member", "graph"), None),
        P(None, "chan"),
        P("chan"),
        P("graph", "chan"),
        P("chan", None),
        P("chan", None),
        P("graph", None, None),
        P(None, "graph", None),
        P(),
    )
    return jax.shard_map(
        on_device,
        mesh=mesh,
        in_specs=placed,
        out_specs=P(("member", "graph"), "chan"),
        check_vma=False,
    )
```

profile of v0, /device:TPU:514, one launch (start us, length us, event | category | flops | bytes accessed | tf_op | source)
XLA Modules:
  0.0 256.0 jit_solution(5669027712290382553)
XLA Ops:
  6.6 0.9 compare_and_fusion
  7.6 14.1 %gather_fusion = bf16[4096,256]{1,0:T(8,128)(2,1)S(1)} fusion(bf16[1024,256]{1,0:T(8,128)(2,1)} %param.13, s32[4096]{0:T(1024)S(1)} %broadcast_clamp_fusion.1), kind=kCustom, calls=%fused_computation | custom fusion | bytes 4210688 | tf_op jit(solution)/shard_map/jit(_take)/gather | solution.py:61
  21.7 0.8 broadcast_select_fusion
  22.5 72.0 %all_to_all.20 = bf16[64,64,256]{2,1,0:T(8,128)(2,1)} all-to-all(bf16[64,64,256]{2,1,0:T(8,128)(2,1)S(1)} %broadcast_select_fusion), channel_id=1, replica_groups=mesh['member'=2,'graph'=64,'chan'=2] {'graph'}, dimensions={0} | all-to-all | bytes 4194304 | tf_op jit(solution)/shard_map/all_to_all | solution.py:64
  94.6 0.7 copy-done.4
  95.4 0.2 dynamic-slice_reduce_fusion
  95.7 0.5 broadcast.108
  96.2 0.7 reduce.9
  97.0 0.2 copy.10
  97.4 25.7 %all-gather.2.cloned.1.call-done = bf16[64,128,256]{2,1,0:T(8,128)(2,1)} async-done(((bf16[64,64,256]{2,1,0:T(8,128)(2,1)}), bf16[64,128,256]{2,1,0:T(8,128)(2,1)}) %all-gather.2.cloned.1.call-update) | async-done | bytes 4194320 | tf_op jit(solution)/shard_map/all_gather | solution.py:65
  123.0 6.1 %multiply_convert_fusion = bf16[8192,256]{1,0:T(8,128)(2,1)} fusion(bf16[8192,256]{1,0:T(8,128)(2,1)} %bitcast.64, bf16[256,256]{1,0:T(8,128)(2,1)S(1)} %copy-done.6, f32[256]{0:T(256)S(1)} %copy-done.8), kind=kOutput, calls=%fused_computation.21 | convolution fusion | flops 1086324736 | bytes 8520704 | tf_op jit(solution)/shard_map/dot_general | solution.py:23
  129.1 9.2 %while.22 = (s32[]{:T(128)}, f32[640,256]{1,0:T(8,128)S(1)}, s32[4,2048]{1,0:T(4,128)S(1)}, bf16[4,2048,256]{2,1,0:T(8,128)(2,1)}, s32[]{:T(128)}, /*index=5*/s32[]{:T(128)}) while((s32[]{:T(128)}, f32[640,256]{1,0:T(8,128)S(1)}, s32[4,2048]{1,0:T(4,128)S(1)}, bf16[4,2048,256]{2,1,0:T(8,128)(2,1)}, s32[]{:T(128)}, ...), condition=%wide.region_1.2_spmd.clone, body=%wide.region_0.1_spmd.clone.sunk | while | flops 672727040 | bytes 2384467 | solution.py:41
  129.1 2.3 fusion.32
  131.4 2.3 fusion.32
  133.8 2.3 fusion.32
  136.1 2.3 fusion.32
  138.4 0.4 fusion.16
  138.8 4.9 %all_to_all.21 = f32[2,640,256]{1,2,0:T(8,128)S(1)} all-to-all(f32[2,640,256]{1,2,0:T(8,128)S(1)} %bitcast.56), channel_id=1, replica_groups=mesh['member'=2,'graph'=64,'chan'=2] {'chan'}, dimensions={0} | all-to-all | bytes 2621440 | tf_op jit(solution)/shard_map/all_to_all | solution.py:17
  143.7 0.1 reduce_sum.18
  143.9 0.4 fusion.18
  144.3 4.3 %all_to_all.22 = f32[2,640,128]{1,2,0:T(8,128)S(1)} all-to-all(f32[2,640,128]{1,2,0:T(8,128)S(1)} %bitcast.58), channel_id=1, replica_groups=mesh['member'=2,'graph'=64,'chan'=2] {'chan'}, dimensions={0} | all-to-all | bytes 1310720 | tf_op jit(solution)/shard_map/all_to_all | solution.py:17
  148.6 0.2 copy.11
  148.8 24.0 %gather_fusion.1 = bf16[8192,128]{1,0:T(8,128)(2,1)S(1)} fusion(bf16[640,128]{1,0:T(8,128)(2,1)S(1)} %copy.11, s32[8192]{0:T(1024)S(1)} %broadcast_clamp_fusion), kind=kCustom, calls=%fused_computation.1 | custom fusion | bytes 4227072 | tf_op jit(solution)/shard_map/jit(_take)/gather | solution.py:77
  172.8 2.6 %broadcast_select_fusion.1 = bf16[64,128,128]{2,1,0:T(8,128)(2,1)} fusion(bf16[64,128,128]{2,1,0:T(8,128)(2,1)S(1)} %bitcast.54, pred[64,128]{1,0:T(8,128)(4,1)S(1)} %compare_and_fusion.1), kind=kLoop, calls=%fused_computation.23 | loop fusion | flops 1048576 | bytes 4202496 | tf_op jit(solution)/shard_map/jit(_take)/select_n | solution.py:77
  175.5 13.7 %all-to-all-start.3 = ((bf16[64,128,128]{2,1,0:T(8,128)(2,1)}), bf16[64,128,128]{2,1,0:T(8,128)(2,1)S(1)}, u32[]{:S(2)}, u32[]{:S(2)}) async-start(bf16[64,128,128]{2,1,0:T(8,128)(2,1)} %broadcast_select_fusion.1), calls=%async_computation.3 | async-start | bytes 4194304 | tf_op jit(solution)/shard_map/all_to_all | solution.py:78
  189.2 52.1 %all-to-all-done.3 = bf16[64,128,128]{2,1,0:T(8,128)(2,1)S(1)} async-done(((bf16[64,128,128]{2,1,0:T(8,128)(2,1)}), bf16[64,128,128]{2,1,0:T(8,128)(2,1)S(1)}, u32[]{:S(2)}, u32[]{:S(2)}) %all-to-all-start.3) | async-done | bytes 2097184 | tf_op jit(solution)/shard_map/all_to_all | solution.py:78
  241.3 7.0 %while.23 = (s32[]{:T(128)}, f32[1024,128]{1,0:T(8,128)S(1)}, s32[4,2048]{1,0:T(4,128)S(1)}, bf16[4,2048,128]{2,1,0:T(8,128)(2,1)S(1)}, s32[]{:T(128)}, /*index=5*/s32[]{:T(128)}) while((s32[]{:T(128)}, f32[1024,128]{1,0:T(8,128)S(1)}, s32[4,2048]{1,0:T(4,128)S(1)}, bf16[4,2048,128]{2,1,0:T(8,128)(2,1)S(1)}, s32[]{:T(128)}, ...), condition=%wide.region_5.6_spmd.clone, body=%wide.region_4.5_spmd.clone.sunk | while | flops 539230208 | bytes 1597527 | solution.py:41
  241.3 1.7 fusion.34
  243.1 1.7 fusion.34
  244.9 1.7 fusion.34
  246.6 1.7 fusion.34
  248.4 0.8 add_convert_fusion.1
  (44 shorter events, 0.7 us)
Async XLA Ops:
  6.5 131.8 %copy-start = (bf16[256,512]{1,0:T(8,128)(2,1)S(1)}, bf16[256,512]{1,0:T(8,128)(2,1)}, u32[]{:S(2)}) copy-start(bf16[256,512]{1,0:T(8,128)(2,1)} %param.17) | copy-start | bytes 786436
  6.6 116.5 %all-gather.2.cloned.1.call-start = ((), (), s32[]{:S(2)}) async-start(), calls=%async_computation.4 | async-start | bytes 6291456 | tf_op jit(solution)/shard_map/all_gather | solution.py:65
  94.5 0.8 copy-start.4
  94.5 0.8 copy-start.5
  94.5 1.7 copy-start.3
  94.5 2.4 copy-start.2
  94.5 28.5 %copy-start.6 = (bf16[256,256]{1,0:T(8,128)(2,1)S(1)}, bf16[256,256]{1,0:T(8,128)(2,1)}, u32[]{:S(2)}) copy-start(bf16[256,256]{1,0:T(8,128)(2,1)} %param.14) | copy-start | bytes 393220
  94.5 28.5 %copy-start.8 = (f32[256]{0:T(256)S(1)}, f32[256]{0:T(256)}, u32[]{:S(2)}) copy-start(f32[256]{0:T(256)} %param.15) | copy-start | bytes 3076
  138.8 5.1 %copy-start.7 = (bf16[256,256]{1,0:T(8,128)(2,1)S(1)}, bf16[256,256]{1,0:T(8,128)(2,1)}, u32[]{:S(2)}) copy-start(bf16[256,256]{1,0:T(8,128)(2,1)} %param.18) | copy-start | bytes 393220
  175.5 65.9 %all-to-all-start.3 = ((bf16[64,128,128]{2,1,0:T(8,128)(2,1)}), bf16[64,128,128]{2,1,0:T(8,128)(2,1)S(1)}, u32[]{:S(2)}, u32[]{:S(2)}) async-start(bf16[64,128,128]{2,1,0:T(8,128)(2,1)} %broadcast_select_fusion.1), calls=%async_computation.3 | async-start | bytes 4194304 | tf_op jit(solution)/shard_map/all_to_all | solution.py:78
  241.3 7.0 %copy-start.1 = (bf16[1024,256]{1,0:T(8,128)(2,1)S(1)}, bf16[1024,256]{1,0:T(8,128)(2,1)}, u32[]{:S(2)}) copy-start(bf16[1024,256]{1,0:T(8,128)(2,1)} %param.13) | copy-start | bytes 1572868
Sparse Core Ops, SparseCore 0:
  94.7 28.2 all-gather.1
where the time goes:
time: 257 us; the launch traced here: 256 us
  blocking collectives  81.2 us (32%)
  waiting for transfers between devices  77.9 us (30%)
  local copies, waits for them, and re-layouts  40.4 us (16%)
  matrix products  22.8 us (9%)
  starting transfers between devices  13.7 us (5%)
  between operations  13.7 us (5%)
  other arithmetic  6.13 us (2%)
    all_to_all x1, blocking collectives, on_device(): lax.all_to_all(picked, 'graph', split_axis=0, concat_axis=0, tiled=True)  72 us
    all_to_all x1, waiting for transfers between devices, on_device(): lax.all_to_all(returned, 'graph', split_axis=0, concat_axis=0, tiled=True)  52.1 us
    all_gather x1, waiting for transfers between devices, on_device(): joined = lax.all_gather(arrived, 'chan', axis=1, tiled=True)  25.7 us
    gather x1, local copies, waits for them, and re-layouts, on_device(): jnp.take(projected, dst_rows, axis=0)  24 us
    dot_general x8, matrix products, add_block(): jnp.dot(one_hot, piece_vals, preferred_element_type=jnp.float32)  15.9 us
    gather x1, local copies, waits for them, and re-layouts, on_device(): jnp.take(grid_state, chosen.reshape(-1), axis=0)  14.1 us
    all_to_all x1, starting transfers between devices, on_device(): lax.all_to_all(returned, 'graph', split_axis=0, concat_axis=0, tiled=True)  13.7 us
    all_to_all x2, blocking collectives, sum_at_owner(): lax.all_to_all(parts, axis, split_axis=0, concat_axis=0, tiled=True)  9.21 us
  transfers between devices with their start and end apart: 2, of which 2 were waited for; matrix products, arithmetic and copies ran while one was open for 1% of the time, Pallas kernels for 0%

commit v1 on v0

--- a/solution.py
+++ b/solution.py
@@ -1,10 +1,20 @@
+import functools
 import math
 
 import jax
 import jax.numpy as jnp
 from jax import lax
+from jax.experimental import pallas as pl
+from jax.experimental.pallas import tpu as pltpu
 from jax.sharding import PartitionSpec as P
 
+MESH_ID = pl.DeviceIdType.MESH
+KEEP = 32
+HALF = KEEP // 2
+REACH = 2
+OWN = 16
+NEAR_ROWS = 256
+CHUNK = 256
 
 def split_up(value, dim, count):
     lengths = value.shape
@@ -44,7 +54,7 @@
     return result
 
 
-def on_device(
+def dense(
     grid_state, w_src, bias_src, mesh_embed, w_node, w_dec, slot_src, slot_dst, slot_count
 ):
     peers = lax.axis_size("graph")
@@ -85,6 +95,329 @@
     return (own_cols.astype(jnp.float32) + decoded).astype(jnp.bfloat16)
 
 
+def silu(v):
+    return v / (1.0 + jnp.exp(-v))
+
+
+def pick_turned(table, idx):
+    rows = table.shape[0]
+    hot = jnp.where(
+        lax.broadcasted_iota(jnp.int32, (rows, idx.shape[1]), 0) == idx, 1.0, 0.0
+    ).astype(jnp.bfloat16)
+    return lax.dot_general(table, hot, (((0,), (0,)), ((), ())), preferred_element_type=jnp.float32)
+
+
+def spread(rows, idx):
+    return jnp.where(
+        lax.broadcasted_iota(jnp.int32, (rows, idx.shape[1]), 0) == idx, 1.0, 0.0
+    ).astype(jnp.bfloat16)
+
+
+def step_kernel(
+    n, hot_ref, grid_ref, wsrc_ref, bias_ref, embed_ref, wnode_ref, wdec_ref,
+    srcx_ref, dstx_ref, hsrc_ref, dst_ref, out_ref,
+    base_out, near_out, base_in, near_in, dst_in, emb_in, part_out, part_in,
+    acc, hid_out, hid_in, prj_out, prj_in, back_out, nback_out, back_in, nback_in, hot_out, hot_in, dec,
+    ssem, rsem,
+):
+    me = lax.axis_index("graph")
+    core = lax.axis_index("chan")
+    other = 1 - core
+    grid_rows = grid_ref.shape[0]
+    mesh_rows = embed_ref.shape[0]
+    owners = mesh_rows // OWN
+    span = cap_near(dst_ref.shape[2])
+    bf = jnp.bfloat16
+
+    barrier = pltpu.get_barrier_semaphore()
+
+    @pl.loop(1, n)
+    def _(i):
+        pl.semaphore_signal(barrier, inc=1, device_id={"graph": lax.rem(me + i, n)}, device_id_type=MESH_ID)
+
+    pl.semaphore_signal(barrier, inc=1, device_id={"chan": other}, device_id_type=MESH_ID)
+
+    def to_graph(src, dst, k, peer):
+        return pltpu.make_async_remote_copy(
+            src_ref=src, dst_ref=dst, send_sem=ssem.at[k], recv_sem=rsem.at[k],
+            device_id={"graph": peer}, device_id_type=MESH_ID)
+
+    def to_core(src, dst, k):
+        return pltpu.make_async_remote_copy(
+            src_ref=src, dst_ref=dst, send_sem=ssem.at[k], recv_sem=rsem.at[k],
+            device_id={"chan": other}, device_id_type=MESH_ID)
+
+    DST, EMB, BASE, NEAR, PART, FWDB, FWDN, HID, PRJ, BACK, NBACK, HOT = range(12)
+
+    @pl.loop(0, (n * HALF) // CHUNK)
+    def _(j):
+        idx = srcx_ref[core, :, pl.ds(pl.multiple_of(j * CHUNK, CHUNK), CHUNK)]
+        rows = pick_turned(grid_ref[...], idx).T.astype(bf)
+        base_out[pl.ds(j * (CHUNK // HALF), CHUNK // HALF)] = rows.reshape(CHUNK // HALF, HALF, rows.shape[1])
+
+    near_out[...] = pick_turned(grid_ref[...], srcx_ref[core, :, n * HALF:]).T.astype(bf)
+    used = (2 * REACH + 1) * span
+    near_in[core, used:, :] = jnp.zeros((NEAR_ROWS - used, near_in.shape[2]), bf)
+
+    pl.semaphore_wait(barrier, n)
+
+    @pl.loop(1, n)
+    def _(i):
+        peer = lax.rem(me + i, n)
+        to_graph(dst_ref.at[peer], dst_in.at[me], DST, peer).start()
+
+    @pl.loop(1, n)
+    def _(i):
+        peer = lax.rem(me + i, n)
+        to_graph(base_out.at[peer], base_in.at[core, me], BASE, peer).start()
+
+    for o in range(-REACH, REACH + 1):
+        rows = pl.ds((o + REACH) * span, span)
+        if o == 0:
+            near_in[core, (o + REACH) * span:(o + REACH + 1) * span] = near_out[(o + REACH) * span:(o + REACH + 1) * span]
+        else:
+            to_graph(near_out.at[rows], near_in.at[core, rows], NEAR, lax.rem(me + o + n, n)).start()
+
+    @pl.loop(0, owners)
+    def _(p):
+        @pl.when(p != me)
+        def _():
+            to_graph(embed_ref.at[pl.ds(p * OWN, OWN)], emb_in.at[me], EMB, p).start()
+
+    base_in[core, pl.ds(me, 1)] = base_out[pl.ds(me, 1)]
+    dst_in[pl.ds(me, 1)] = dst_ref[pl.ds(me, 1)]
+
+    to_graph(dst_ref.at[pl.ds(0, n - 1)], dst_in.at[pl.ds(0, n - 1)], DST, me).wait_recv()
+    hot = hot_ref[0]
+    live = lax.broadcasted_iota(jnp.int32, (1, dst_ref.shape[2]), 1) < hot_ref[1]
+    hot_dst = jnp.where(live, dst_in[hot], -1)
+    hot_src = hsrc_ref[...]
+    rows = pick_turned(grid_ref[...], hot_src).T.astype(bf)
+    msgs = silu(jnp.dot(rows, wsrc_ref[...], preferred_element_type=jnp.float32) + bias_ref[...]).astype(bf)
+    part = jnp.dot(spread(mesh_rows, hot_dst), msgs, preferred_element_type=jnp.float32).astype(bf)
+    part_out[...] = part.reshape(owners, OWN, part.shape[1])
+
+    @pl.loop(0, owners)
+    def _(p):
+        @pl.when(p != me)
+        def _():
+            to_graph(part_out.at[p], part_in.at[me], PART, p).start()
+
+    def wait_in(ref, k):
+        to_graph(ref, ref, k, me).wait_recv()
+
+    wait_in(base_in.at[core, pl.ds(0, n - 1)], BASE)
+    to_core(base_in.at[core], base_in.at[core], FWDB).start()
+    wait_in(near_in.at[core, pl.ds(0, 2 * REACH * span)], NEAR)
+    to_core(near_in.at[core], near_in.at[core], FWDN).start()
+
+    acc[...] = jnp.zeros_like(acc)
+
+    def add_rows(rows, idx):
+        m = silu(jnp.dot(rows, wsrc_ref[...], preferred_element_type=jnp.float32) + bias_ref[...]).astype(bf)
+        acc[0:mesh_rows] += jnp.dot(spread(mesh_rows, idx), m, preferred_element_type=jnp.float32)
+
+    def add_half(h):
+        @pl.loop(0, (n * HALF) // CHUNK)
+        def _(j):
+            rows = base_in[h, pl.ds(j * (CHUNK // HALF), CHUNK // HALF)].reshape(CHUNK, base_in.shape[3])
+            add_rows(rows, dstx_ref[h, :, pl.ds(pl.multiple_of(j * CHUNK, CHUNK), CHUNK)])
+        add_rows(near_in[h], dstx_ref[h, :, n * HALF:])
+
+    add_half(core)
+    to_core(base_in.at[other], base_in.at[other], FWDB).wait_recv()
+    to_core(near_in.at[other], near_in.at[other], FWDN).wait_recv()
+    add_half(other)
+
+    @pl.when(me < owners)
+    def _():
+        wait_in(part_in.at[pl.ds(0, n - 1)], PART)
+        wait_in(emb_in.at[pl.ds(0, n - 1)], EMB)
+        part_in[pl.ds(me, 1)] = part_out[pl.ds(me, 1)]
+        emb_in[pl.ds(me, 1)] = embed_ref[pl.ds(me * OWN, OWN)].reshape(1, OWN, embed_ref.shape[1])
+        acc[mesh_rows:mesh_rows + OWN] = part_in[...].astype(jnp.float32).sum(axis=0)
+
+    half = hid_out.shape[1]
+    agg = acc[...].astype(bf)
+    hid_out[...] = jnp.dot(agg, wnode_ref[:, pl.ds(pl.multiple_of(other * half, half), half)], preferred_element_type=jnp.float32)
+    send = to_core(hid_out, hid_in, HID)
+    send.start()
+    own = jnp.dot(agg, wnode_ref[:, pl.ds(pl.multiple_of(core * half, half), half)], preferred_element_type=jnp.float32)
+    send.wait_recv()
+    nodes = silu(own + hid_in[...])
+    quarter = prj_out.shape[1]
+    lat = (embed_ref[...].astype(jnp.float32) + nodes[0:mesh_rows]).astype(bf)
+    hot_lat = (emb_in[hot].astype(jnp.float32) + nodes[mesh_rows:]).astype(bf)
+    w_other = wdec_ref[:, pl.ds(pl.multiple_of(other * quarter, quarter), quarter)]
+    w_own = wdec_ref[:, pl.ds(pl.multiple_of(core * quarter, quarter), quarter)]
+    prj_out[0:mesh_rows] = jnp.dot(lat, w_other, preferred_element_type=jnp.float32)
+    prj_out[mesh_rows:] = jnp.dot(hot_lat, w_other, preferred_element_type=jnp.float32)
+    send2 = to_core(prj_out, prj_in, PRJ)
+    send2.start()
+    own_p = jnp.dot(lat, w_own, preferred_element_type=jnp.float32)
+    own_h = jnp.dot(hot_lat, w_own, preferred_element_type=jnp.float32)
+    send2.wait_recv()
+    proj = (own_p + prj_in[0:mesh_rows]).astype(bf)
+    hot_out[...] = (own_h + prj_in[mesh_rows:]).astype(bf)
+
+    @pl.when(me < owners)
+    def _():
+        @pl.loop(1, n)
+        def _(i):
+            peer = lax.rem(me + i, n)
+            to_graph(hot_out, hot_in.at[me], HOT, peer).start()
+
+    for h in range(2):
+        @pl.loop(0, (n * HALF) // CHUNK)
+        def _(j):
+            idx = dstx_ref[h, :, pl.ds(pl.multiple_of(j * CHUNK, CHUNK), CHUNK)]
+            rows = pick_turned(proj, idx).T.astype(bf)
+            back_out[h, pl.ds(j * (CHUNK // HALF), CHUNK // HALF)] = rows.reshape(CHUNK // HALF, HALF, rows.shape[1])
+        nback_out[h] = pick_turned(proj, dstx_ref[h, :, n * HALF:]).T.astype(bf)
+
+    @pl.loop(1, n)
+    def _(i):
+        peer = lax.rem(me + i, n)
+        to_graph(back_out.at[:, peer], back_in.at[:, me], BACK, peer).start()
+
+    for h in range(2):
+        for o in range(-REACH, REACH + 1):
+            a = (o + REACH) * span
+            if o == 0:
+                nback_in[h, a:a + span] = nback_out[h, a:a + span]
+            else:
+                to_graph(nback_out.at[h, pl.ds(a, span)], nback_in.at[h, pl.ds(a, span)], NBACK, lax.rem(me - o + n, n)).start()
+        nback_in[h, used:, :] = jnp.zeros((NEAR_ROWS - used, nback_in.shape[2]), bf)
+    for h in range(2):
+        back_in[h, pl.ds(me, 1)] = back_out[h, pl.ds(me, 1)]
+
+    dec[...] = grid_ref[:, pl.ds(pl.multiple_of(core * quarter, quarter), quarter)].astype(jnp.float32)
+    wait_in(nback_in.at[:, pl.ds(0, 2 * REACH * span)], NBACK)
+    for h in range(2):
+        dec[...] += jnp.dot(spread(grid_rows, srcx_ref[h, :, n * HALF:]), nback_in[h], preferred_element_type=jnp.float32)
+
+    @pl.when(me < owners)
+    def _():
+        wait_in(hot_in.at[pl.ds(0, owners - 1)], HOT)
+        hot_in[pl.ds(me, 1)] = hot_out[...].reshape(1, OWN, quarter)
+
+    @pl.when(me >= owners)
+    def _():
+        wait_in(hot_in, HOT)
+
+    hot_rows = pick_turned(hot_in[...].reshape(mesh_rows, quarter), hot_dst).astype(bf)
+    dec[...] += lax.dot_general(spread(grid_rows, hot_src), hot_rows, (((1,), (1,)), ((), ())), preferred_element_type=jnp.float32)
+
+    wait_in(back_in.at[:, pl.ds(0, n - 1)], BACK)
+    for h in range(2):
+        @pl.loop(0, (n * HALF) // CHUNK)
+        def _(j):
+            rows = back_in[h, pl.ds(j * (CHUNK // HALF), CHUNK // HALF)].reshape(CHUNK, quarter)
+            idx = srcx_ref[h, :, pl.ds(pl.multiple_of(j * CHUNK, CHUNK), CHUNK)]
+            dec[...] += jnp.dot(spread(grid_rows, idx), rows, preferred_element_type=jnp.float32)
+
+    out_ref[...] = dec[...].astype(bf)
+
+    def wait_out(ref, k):
+        to_graph(ref, ref, k, me).wait_send()
+
+    wait_out(dst_ref.at[pl.ds(0, n - 1)], DST)
+    wait_out(base_out.at[pl.ds(0, n - 1)], BASE)
+    wait_out(near_out.at[pl.ds(0, 2 * REACH * span)], NEAR)
+
+    @pl.when(me < owners)
+    def _():
+        wait_out(embed_ref.at[pl.ds(0, mesh_rows - OWN)], EMB)
+        wait_out(part_out.at[pl.ds(0, owners - 1)], PART)
+        wait_out(back_out.at[0, pl.ds(0, n - 1)], HOT)
+
+    @pl.when(me >= owners)
+    def _():
+        wait_out(embed_ref, EMB)
+        wait_out(part_out, PART)
+
+    to_core(base_in.at[core], base_in.at[core], FWDB).wait_send()
+    to_core(near_in.at[core], near_in.at[core], FWDN).wait_send()
+    send.wait_send()
+    send2.wait_send()
+    wait_out(back_out.at[:, pl.ds(0, n - 1)], BACK)
+    wait_out(nback_out.at[:, pl.ds(0, 2 * REACH * span)], NBACK)
+
+
+def cap_near(capacity):
+    return (capacity - KEEP) // 2
+
+
+def halves(table):
+    return table.reshape(table.shape[0], 2, HALF).transpose(1, 0, 2).reshape(2, -1)
+
+
+def near_halves(table, span):
+    rows = table.reshape(2 * REACH + 1, 2, span).transpose(1, 0, 2).reshape(2, -1)
+    return jnp.pad(rows, ((0, 0), (0, NEAR_ROWS - rows.shape[1])), constant_values=-1)
+
+
+def around(table, middle):
+    ring = jnp.concatenate([table[-REACH:], table, table[:REACH]], axis=0)
+    return lax.dynamic_slice_in_dim(ring, middle, 2 * REACH + 1, 0)
+
+
+def compact(hot, grid_state, w_src, bias_src, mesh_embed, w_node, w_dec, slot_src, slot_dst, slot_count):
+    n = lax.axis_size("graph")
+    me = lax.axis_index("graph")
+    capacity = slot_src.shape[2]
+    span = cap_near(capacity)
+    pos = jnp.arange(capacity, dtype=jnp.int32)[None, :]
+    ids = jnp.arange(n, dtype=jnp.int32)[:, None]
+    sent = lax.dynamic_slice_in_dim(slot_count, me, 1, 0).reshape(n, 1)
+    came = lax.dynamic_slice_in_dim(slot_count, me, 1, 1)
+    src_live = jnp.where(pos < sent, slot_src[0], -1)
+    src = jnp.where(ids != hot, src_live, -1)
+    dst = jnp.where((pos < came) & (me != hot), slot_dst[:, 0, :], -1)
+    srcx = jnp.concatenate([halves(src[:, :KEEP]), near_halves(around(src, me)[:, KEEP:], span)], axis=1)[:, None, :]
+    dstx = jnp.concatenate([halves(dst[:, :KEEP]), near_halves(around(dst, me)[::-1, KEEP:], span)], axis=1)[:, None, :]
+    hsrc = lax.dynamic_slice_in_dim(src_live, hot, 1, 0)
+    hot_info = jnp.stack([hot, lax.dynamic_slice(slot_count, (me, hot), (1, 1))[0, 0]]).astype(jnp.int32)
+    grid_rows, width = grid_state.shape
+    mesh_rows, half = mesh_embed.shape
+    quarter = width // 2
+    owners = mesh_rows // OWN
+    bf, f32 = jnp.bfloat16, jnp.float32
+    vm = pltpu.VMEM
+    return pl.pallas_call(
+        functools.partial(step_kernel, n),
+        out_shape=jax.ShapeDtypeStruct((grid_rows, quarter), bf),
+        in_specs=[pl.BlockSpec(memory_space=pltpu.SMEM)] + [pl.BlockSpec(memory_space=vm)] * 10,
+        out_specs=pl.BlockSpec(memory_space=vm),
+        scratch_shapes=[
+            vm((n, HALF, width), bf), vm((NEAR_ROWS, width), bf),
+            vm((2, n, HALF, width), bf), vm((2, NEAR_ROWS, width), bf),
+            vm((n, 1, capacity), jnp.int32), vm((n, OWN, half), bf),
+            vm((owners, OWN, half), bf), vm((n, OWN, half), bf),
+            vm((mesh_rows + OWN, half), f32),
+            vm((mesh_rows + OWN, half), f32), vm((mesh_rows + OWN, half), f32),
+            vm((mesh_rows + OWN, quarter), f32), vm((mesh_rows + OWN, quarter), f32),
+            vm((2, n, HALF, quarter), bf), vm((2, NEAR_ROWS, quarter), bf),
+            vm((2, n, HALF, quarter), bf), vm((2, NEAR_ROWS, quarter), bf),
+            vm((OWN, quarter), bf), vm((owners, OWN, quarter), bf),
+            vm((grid_rows, quarter), f32),
+            pltpu.SemaphoreType.DMA((12,)), pltpu.SemaphoreType.DMA((12,)),
+        ],
+        compiler_params=pltpu.CompilerParams(collective_id=0, has_side_effects=True, vmem_limit_bytes=48 * 1024 * 1024),
+    )(hot_info, grid_state, w_src, bias_src[None, :], mesh_embed, w_node, w_dec, srcx, dstx, hsrc, slot_dst)
+
+
+def on_device(grid_state, w_src, bias_src, mesh_embed, w_node, w_dec, slot_src, slot_dst, slot_count):
+    args = (grid_state, w_src, bias_src, mesh_embed, w_node, w_dec, slot_src, slot_dst, slot_count)
+    n = slot_count.shape[0]
+    apart = jnp.abs(jnp.arange(n)[:, None] - jnp.arange(n)[None, :])
+    far = jnp.minimum(apart, n - apart) > REACH
+    over = jnp.any(far & (slot_count > KEEP), axis=0)
+    hot = jnp.argmax(over).astype(jnp.int32)
+    fits = jnp.sum(over.astype(jnp.int32)) <= 1
+    return lax.cond(fits, lambda: compact(hot, *args), lambda: dense(*args))
+
+
 def solution(mesh):
     placed = (
         P(("member", "graph"), None),

time: 257 us -> 126 us (0.49)
  the two profiles are of different devices: /device:TPU:514 before, /device:TPU:652 now
where the time goes in v1:
time: 126 us
  Pallas kernels  100 us (79%)
  between operations  14.1 us (11%)
  other arithmetic  5.78 us (5%)
  local copies, waits for them, and re-layouts  3.43 us (3%)
  loops' own time  2.62 us (2%)
    pallas_call x1, Pallas kernels, compact(): pl.pallas_call(functools.partial(step_kernel, n), out_shape=jax.ShapeDtyp...  100 us
    another operation x1, loops' own time, on_device(): return lax.cond(fits, lambda: compact(hot, *args), lambda: dense(*args))  2.62 us

profile of v1, /device:TPU:652, one launch (start us, length us, event | category | flops | bytes accessed | tf_op | source)
XLA Modules:
  0.0 126.0 jit_solution(8892277316718253658)
XLA Ops:
  6.5 0.8 fusion.32
  7.3 0.6 convert_reduce_fusion
  8.6 0.7 iota_reduce_fusion
  9.4 109.1 %conditional.1 = (bf16[1024,128]{1,0:T(8,128)(2,1)S(1)}) conditional(s32[]{:T(128)} %convert_element_type.30, (bf16[1024,256]{1,0:T(8,128)(2,1)}, s32[64,64]{1,0:T(8,128)}, s32[1,64,128]{2,1,0:T(8,128)}, s32[64,1,128]{2,1,0:T(1,128)}, bf16[640,256]{1,0:T(8,128)(2,1)}, /*index=5*/bf16[256,256]{1,0:T(8,128)(2,1)}, f32[256]{0:T(256)}, ...), branch_computations={%region_3.10_spmd, %region_10.11_spmd} | conditional | flops 2554142720 | bytes 78037800 | solution.py:418
  9.4 0.8 copy.38
  10.8 0.8 fusion.17
  11.6 0.2 dynamic-slice_reduce_fusion
  11.8 0.6 iota_compare_fusion.11
  12.4 0.8 broadcast_select_fusion
  13.3 0.1 slice.23
  13.4 0.1 reshape.159
  13.5 0.1 reshape.160
  13.6 0.1 copy.31
  13.6 0.1 copy.32
  13.7 0.1 reshape.158
  13.8 0.1 slice.19
  13.9 0.1 reshape.155
  14.0 0.1 reshape.156
  14.1 0.1 copy.28
  14.1 0.1 copy.29
  14.2 0.1 reshape.154
  16.1 0.7 dynamic_slice.39
  16.8 1.3 %pad_add_fusion.hot_ref = s32[2]{0:T(128)S(1)} fusion(s32[1]{0:T(128)} %bitcast.18, s32[1]{0:T(128)} %bitcast.17), kind=kLoop, calls=%fused_computation.45 | loop fusion | flops 2 | bytes 16 | tf_op jit(solution)/shard_map/cond/branch_1_fun/stack | solution.py:380
  18.1 100.1 %branch_1_fun.1 = bf16[1024,128]{1,0:T(8,128)(2,1)S(1)} custom-call(s32[2]{0:T(128)S(1)} %pad_add_fusion.hot_ref, bf16[1024,256]{1,0:T(8,128)(2,1)} %get-tuple-element.111.grid_ref, bf16[256,256]{1,0:T(8,128)(2,1)} %get-tuple-element.112.wsrc_ref, f32[1,256]{1,0:T(1,128)} %bitcast.99, bf16[640,256]{1,0:T(8,128)(2,1)} %get-tuple-element.114.embed_ref, ...), custom_call_target="tpu_custom_call" | custom-call | tf_op jit(solution)/shard_map/cond/branch_1_fun/pallas_call | solution.py:387
  118.4 0.7 copy.66
  (12 shorter events, 0.1 us)

commit v2 on v1

--- a/solution.py
+++ b/solution.py
@@ -72,7 +72,12 @@
         peers, half_slots, grid_state.shape[1]
     )
     arrived = lax.all_to_all(picked, "graph", split_axis=0, concat_axis=0, tiled=True)
-    joined = lax.all_gather(arrived, "chan", axis=1, tiled=True)
+    partner = lax.ppermute(arrived, "chan", [(0, 1), (1, 0)])
+    joined = jnp.where(
+        core_index == 0,
+        jnp.concatenate([arrived, partner], axis=1),
+        jnp.concatenate([partner, arrived], axis=1),
+    )
     messages = edge_network(joined.reshape(peers * capacity, grid_state.shape[1]), w_src, bias_src)
     arrive_ok = (positions[None, :] < recv_counts[:, None]).reshape(-1)
     dst_rows = slot_dst[:, 0, :].reshape(-1)
@@ -115,7 +120,8 @@
 
 def step_kernel(
     n, hot_ref, grid_ref, wsrc_ref, bias_ref, embed_ref, wnode_ref, wdec_ref,
-    srcx_ref, dstx_ref, hsrc_ref, dst_ref, out_ref,
+    src_ref, dst_ref, count_ref, out_ref,
+    src_live, dst_live, srcx_ref, dstx_ref,
     base_out, near_out, base_in, near_in, dst_in, emb_in, part_out, part_in,
     acc, hid_out, hid_in, prj_out, prj_in, back_out, nback_out, back_in, nback_in, hot_out, hot_in, dec,
     ssem, rsem,
@@ -149,13 +155,47 @@
 
     DST, EMB, BASE, NEAR, PART, FWDB, FWDN, HID, PRJ, BACK, NBACK, HOT = range(12)
 
-    @pl.loop(0, (n * HALF) // CHUNK)
+    blocks = (n * HALF) // CHUNK
+    capacity = dst_ref.shape[2]
+    with jax.named_scope("index"):
+        hot = hot_ref[0]
+        ids = lax.broadcasted_iota(jnp.int32, (n, n), 0)
+        cols = lax.broadcasted_iota(jnp.int32, (n, n), 1)
+        counts = count_ref[...]
+        sent = jnp.where(ids == me, counts, 0).sum(axis=0, keepdims=True)
+        sent = jnp.where(ids == cols, sent, 0).sum(axis=1, keepdims=True)
+        came = jnp.where(cols == me, counts, 0).sum(axis=1, keepdims=True)
+        pos = lax.broadcasted_iota(jnp.int32, (n, capacity), 1)
+        src_all = jnp.where(pos < sent, src_ref[0] + 1, 0).astype(jnp.float32)
+        src_live[...] = src_all
+        came = jnp.where(me == hot, 0, came)
+        dst_all = jnp.where(pos < came, dst_ref[:, 0, :] + 1, 0).astype(jnp.float32)
+        dst_live[...] = dst_all
+        rows_id = lax.broadcasted_iota(jnp.int32, (n, capacity), 0)
+        src_all = jnp.where(rows_id == hot, 0.0, src_all)
+        near_id = lax.broadcasted_iota(jnp.int32, (8, capacity), 0)
+        near_src = jnp.zeros((8, capacity), jnp.float32)
+        near_dst = jnp.zeros((8, capacity), jnp.float32)
+        for o in range(-REACH, REACH + 1):
+            to = lax.rem(me + o + n, n)
+            row = jnp.where(to == hot, 0.0, src_live[pl.ds(to, 1)])
+            near_src = jnp.where(near_id == o + REACH, row, near_src)
+            near_dst = jnp.where(near_id == o + REACH, dst_live[pl.ds(lax.rem(me - o + n, n), 1)], near_dst)
+        for h in range(2):
+            base = base_layout(capacity, h)
+            srcx_ref[h, 0:blocks] = lay_out(src_all, *base)
+            dstx_ref[h, 0:blocks] = lay_out(dst_all, *base)
+            near = near_layout(capacity, h)
+            srcx_ref[h, blocks:] = lay_out(near_src, *near)[:, 0:CHUNK]
+            dstx_ref[h, blocks:] = lay_out(near_dst, *near)[:, 0:CHUNK]
+
+    @pl.loop(0, blocks)
     def _(j):
-        idx = srcx_ref[core, :, pl.ds(pl.multiple_of(j * CHUNK, CHUNK), CHUNK)]
+        idx = srcx_ref[core, pl.ds(j, 1)]
         rows = pick_turned(grid_ref[...], idx).T.astype(bf)
         base_out[pl.ds(j * (CHUNK // HALF), CHUNK // HALF)] = rows.reshape(CHUNK // HALF, HALF, rows.shape[1])
 
-    near_out[...] = pick_turned(grid_ref[...], srcx_ref[core, :, n * HALF:]).T.astype(bf)
+    near_out[...] = pick_turned(grid_ref[...], srcx_ref[core, blocks:]).T.astype(bf)
     used = (2 * REACH + 1) * span
     near_in[core, used:, :] = jnp.zeros((NEAR_ROWS - used, near_in.shape[2]), bf)
 
@@ -188,10 +228,8 @@
     dst_in[pl.ds(me, 1)] = dst_ref[pl.ds(me, 1)]
 
     to_graph(dst_ref.at[pl.ds(0, n - 1)], dst_in.at[pl.ds(0, n - 1)], DST, me).wait_recv()
-    hot = hot_ref[0]
-    live = lax.broadcasted_iota(jnp.int32, (1, dst_ref.shape[2]), 1) < hot_ref[1]
-    hot_dst = jnp.where(live, dst_in[hot], -1)
-    hot_src = hsrc_ref[...]
+    hot_src = src_live[pl.ds(hot, 1)].astype(jnp.int32) - 1
+    hot_dst = jnp.where(hot_src >= 0, dst_in[hot], -1)
     rows = pick_turned(grid_ref[...], hot_src).T.astype(bf)
     msgs = silu(jnp.dot(rows, wsrc_ref[...], preferred_element_type=jnp.float32) + bias_ref[...]).astype(bf)
     part = jnp.dot(spread(mesh_rows, hot_dst), msgs, preferred_element_type=jnp.float32).astype(bf)
@@ -218,11 +256,11 @@
         acc[0:mesh_rows] += jnp.dot(spread(mesh_rows, idx), m, preferred_element_type=jnp.float32)
 
     def add_half(h):
-        @pl.loop(0, (n * HALF) // CHUNK)
+        @pl.loop(0, blocks)
         def _(j):
             rows = base_in[h, pl.ds(j * (CHUNK // HALF), CHUNK // HALF)].reshape(CHUNK, base_in.shape[3])
-            add_rows(rows, dstx_ref[h, :, pl.ds(pl.multiple_of(j * CHUNK, CHUNK), CHUNK)])
-        add_rows(near_in[h], dstx_ref[h, :, n * HALF:])
+            add_rows(rows, dstx_ref[h, pl.ds(j, 1)])
+        add_rows(near_in[h], dstx_ref[h, blocks:])
 
     add_half(core)
     to_core(base_in.at[other], base_in.at[other], FWDB).wait_recv()
@@ -268,12 +306,12 @@
             to_graph(hot_out, hot_in.at[me], HOT, peer).start()
 
     for h in range(2):
-        @pl.loop(0, (n * HALF) // CHUNK)
+        @pl.loop(0, blocks)
         def _(j):
-            idx = dstx_ref[h, :, pl.ds(pl.multiple_of(j * CHUNK, CHUNK), CHUNK)]
+            idx = dstx_ref[h, pl.ds(j, 1)]
             rows = pick_turned(proj, idx).T.astype(bf)
             back_out[h, pl.ds(j * (CHUNK // HALF), CHUNK // HALF)] = rows.reshape(CHUNK // HALF, HALF, rows.shape[1])
-        nback_out[h] = pick_turned(proj, dstx_ref[h, :, n * HALF:]).T.astype(bf)
+        nback_out[h] = pick_turned(proj, dstx_ref[h, blocks:]).T.astype(bf)
 
     @pl.loop(1, n)
     def _(i):
@@ -294,7 +332,7 @@
     dec[...] = grid_ref[:, pl.ds(pl.multiple_of(core * quarter, quarter), quarter)].astype(jnp.float32)
     wait_in(nback_in.at[:, pl.ds(0, 2 * REACH * span)], NBACK)
     for h in range(2):
-        dec[...] += jnp.dot(spread(grid_rows, srcx_ref[h, :, n * HALF:]), nback_in[h], preferred_element_type=jnp.float32)
+        dec[...] += jnp.dot(spread(grid_rows, srcx_ref[h, blocks:]), nback_in[h], preferred_element_type=jnp.float32)
 
     @pl.when(me < owners)
     def _():
@@ -310,10 +348,10 @@
 
     wait_in(back_in.at[:, pl.ds(0, n - 1)], BACK)
     for h in range(2):
-        @pl.loop(0, (n * HALF) // CHUNK)
+        @pl.loop(0, blocks)
         def _(j):
             rows = back_in[h, pl.ds(j * (CHUNK // HALF), CHUNK // HALF)].reshape(CHUNK, quarter)
-            idx = srcx_ref[h, :, pl.ds(pl.multiple_of(j * CHUNK, CHUNK), CHUNK)]
+            idx = srcx_ref[h, pl.ds(j, 1)]
             dec[...] += jnp.dot(spread(grid_rows, idx), rows, preferred_element_type=jnp.float32)
 
     out_ref[...] = dec[...].astype(bf)
@@ -348,36 +386,46 @@
     return (capacity - KEEP) // 2
 
 
-def halves(table):
-    return table.reshape(table.shape[0], 2, HALF).transpose(1, 0, 2).reshape(2, -1)
-
-
-def near_halves(table, span):
-    rows = table.reshape(2 * REACH + 1, 2, span).transpose(1, 0, 2).reshape(2, -1)
-    return jnp.pad(rows, ((0, 0), (0, NEAR_ROWS - rows.shape[1])), constant_values=-1)
-
-
-def around(table, middle):
-    ring = jnp.concatenate([table[-REACH:], table, table[:REACH]], axis=0)
-    return lax.dynamic_slice_in_dim(ring, middle, 2 * REACH + 1, 0)
+def lay_out(table, take, mark):
+    high = jnp.floor(table * (1.0 / 32.0))
+    low = table - 32.0 * high
+    dot = functools.partial(jnp.dot, preferred_element_type=jnp.float32)
+    moved = 32.0 * dot(high.astype(jnp.bfloat16), take) + dot(low.astype(jnp.bfloat16), take)
+    group = mark.shape[0]
+    moved = moved.reshape(table.shape[0] // group, group, take.shape[1])
+    return (moved * mark[None]).sum(axis=1).astype(jnp.int32) - 1
+
+
+def base_layout(capacity, h):
+    shape = (capacity, CHUNK)
+    lane = lax.broadcasted_iota(jnp.int32, shape, 1)
+    slot = lax.broadcasted_iota(jnp.int32, shape, 0)
+    take = jnp.where(slot == h * HALF + (lane & (HALF - 1)), 1.0, 0.0).astype(jnp.bfloat16)
+    group = CHUNK // HALF
+    lane = lax.broadcasted_iota(jnp.int32, (group, CHUNK), 1)
+    row = lax.broadcasted_iota(jnp.int32, (group, CHUNK), 0)
+    return take, jnp.where(row * HALF <= lane, 1.0, 0.0) * jnp.where(lane < row * HALF + HALF, 1.0, 0.0)
+
+
+def near_layout(capacity, h):
+    span = cap_near(capacity)
+    count = 2 * REACH + 1
+    shape = (capacity, NEAR_ROWS)
+    lane = lax.broadcasted_iota(jnp.int32, shape, 1)
+    slot = lax.broadcasted_iota(jnp.int32, shape, 0)
+    within = lane
+    for i in range(1, count + 1):
+        within = within - jnp.where(lane >= i * span, span, 0)
+    take = jnp.where(slot == KEEP + h * span + within, 1.0, 0.0).astype(jnp.bfloat16)
+    lane = lax.broadcasted_iota(jnp.int32, (8, NEAR_ROWS), 1)
+    row = lax.broadcasted_iota(jnp.int32, (8, NEAR_ROWS), 0)
+    inside = jnp.where(row * span <= lane, 1.0, 0.0) * jnp.where(lane < row * span + span, 1.0, 0.0)
+    return take, inside * jnp.where(row < count, 1.0, 0.0)
 
 
 def compact(hot, grid_state, w_src, bias_src, mesh_embed, w_node, w_dec, slot_src, slot_dst, slot_count):
     n = lax.axis_size("graph")
-    me = lax.axis_index("graph")
     capacity = slot_src.shape[2]
-    span = cap_near(capacity)
-    pos = jnp.arange(capacity, dtype=jnp.int32)[None, :]
-    ids = jnp.arange(n, dtype=jnp.int32)[:, None]
-    sent = lax.dynamic_slice_in_dim(slot_count, me, 1, 0).reshape(n, 1)
-    came = lax.dynamic_slice_in_dim(slot_count, me, 1, 1)
-    src_live = jnp.where(pos < sent, slot_src[0], -1)
-    src = jnp.where(ids != hot, src_live, -1)
-    dst = jnp.where((pos < came) & (me != hot), slot_dst[:, 0, :], -1)
-    srcx = jnp.concatenate([halves(src[:, :KEEP]), near_halves(around(src, me)[:, KEEP:], span)], axis=1)[:, None, :]
-    dstx = jnp.concatenate([halves(dst[:, :KEEP]), near_halves(around(dst, me)[::-1, KEEP:], span)], axis=1)[:, None, :]
-    hsrc = lax.dynamic_slice_in_dim(src_live, hot, 1, 0)
-    hot_info = jnp.stack([hot, lax.dynamic_slice(slot_count, (me, hot), (1, 1))[0, 0]]).astype(jnp.int32)
     grid_rows, width = grid_state.shape
     mesh_rows, half = mesh_embed.shape
     quarter = width // 2
@@ -387,9 +435,11 @@
     return pl.pallas_call(
         functools.partial(step_kernel, n),
         out_shape=jax.ShapeDtypeStruct((grid_rows, quarter), bf),
-        in_specs=[pl.BlockSpec(memory_space=pltpu.SMEM)] + [pl.BlockSpec(memory_space=vm)] * 10,
+        in_specs=[pl.BlockSpec(memory_space=pltpu.SMEM)] + [pl.BlockSpec(memory_space=vm)] * 9,
         out_specs=pl.BlockSpec(memory_space=vm),
         scratch_shapes=[
+            vm((n, capacity), f32), vm((n, capacity), f32),
+            vm((2, n * HALF // CHUNK + 1, CHUNK), jnp.int32), vm((2, n * HALF // CHUNK + 1, CHUNK), jnp.int32),
             vm((n, HALF, width), bf), vm((NEAR_ROWS, width), bf),
             vm((2, n, HALF, width), bf), vm((2, NEAR_ROWS, width), bf),
             vm((n, 1, capacity), jnp.int32), vm((n, OWN, half), bf),
@@ -404,7 +454,7 @@
             pltpu.SemaphoreType.DMA((12,)), pltpu.SemaphoreType.DMA((12,)),
         ],
         compiler_params=pltpu.CompilerParams(collective_id=0, has_side_effects=True, vmem_limit_bytes=48 * 1024 * 1024),
-    )(hot_info, grid_state, w_src, bias_src[None, :], mesh_embed, w_node, w_dec, srcx, dstx, hsrc, slot_dst)
+    )(hot, grid_state, w_src, bias_src[None, :], mesh_embed, w_node, w_dec, slot_src, slot_dst, slot_count)
 
 
 def on_device(grid_state, w_src, bias_src, mesh_embed, w_node, w_dec, slot_src, slot_dst, slot_count):
@@ -412,9 +462,12 @@
     n = slot_count.shape[0]
     apart = jnp.abs(jnp.arange(n)[:, None] - jnp.arange(n)[None, :])
     far = jnp.minimum(apart, n - apart) > REACH
-    over = jnp.any(far & (slot_count > KEEP), axis=0)
-    hot = jnp.argmax(over).astype(jnp.int32)
-    fits = jnp.sum(over.astype(jnp.int32)) <= 1
+    over = far & (slot_count > KEEP)
+    column = jnp.broadcast_to(jnp.arange(n, dtype=jnp.int32)[None, :], (n, n))
+    last = jnp.max(jnp.where(over, column, 0))
+    first = jnp.min(jnp.where(over, column, n))
+    fits = last <= first
+    hot = last.reshape(1)
     return lax.cond(fits, lambda: compact(hot, *args), lambda: dense(*args))
 
 

time: 126 us -> 105 us (0.83)
  the two profiles are of different devices: /device:TPU:652 before, /device:TPU:640 now
where the time goes in v2:
time: 105 us; the launch traced here: 103 us
  Pallas kernels  99 us (94%)
  other arithmetic  1.49 us (1%)
  between operations  1.3 us (1%)
    pallas_call x1, Pallas kernels, compact(): pl.pallas_call(functools.partial(step_kernel, n), out_shape=jax.ShapeDtyp...  99 us

profile of v2, /device:TPU:640, one launch (start us, length us, event | category | flops | bytes accessed | tf_op | source)
XLA Modules:
  0.0 102.7 jit_solution(3446050366382085286)
XLA Ops:
  0.0 1.5 %select_reduce_fusion = (s32[]{:T(128)}, s32[]{:T(128)}) fusion(s32[64,64]{1,0:T(8,128)} %param.23), kind=kLoop, calls=%fused_computation.52 | loop fusion | flops 45054 | bytes 16392 | tf_op jit(solution)/shard_map/reduce_min | solution.py:468
  2.8 99.2 %conditional.1 = (bf16[1024,128]{1,0:T(8,128)(2,1)S(1)}) conditional(s32[]{:T(128)} %convert_element_type.26, (bf16[1024,256]{1,0:T(8,128)(2,1)}, s32[64,64]{1,0:T(8,128)}, s32[1,64,128]{2,1,0:T(8,128)}, s32[64,1,128]{2,1,0:T(1,128)}, bf16[640,256]{1,0:T(8,128)(2,1)}, /*index=5*/bf16[256,256]{1,0:T(8,128)(2,1)}, f32[256]{0:T(256)}, ...), branch_computations={%region_2.9_spmd, %region_9.10_spmd} | conditional | flops 2573017088 | bytes 80659304 | solution.py:471
  3.0 99.0 %branch_1_fun.1 = bf16[1024,128]{1,0:T(8,128)(2,1)S(1)} custom-call(s32[1]{0:T(128)} %bitcast.17.hot_ref, bf16[1024,256]{1,0:T(8,128)(2,1)} %get-tuple-element.110.grid_ref, bf16[256,256]{1,0:T(8,128)(2,1)} %get-tuple-element.111.wsrc_ref, f32[1,256]{1,0:T(1,128)} %bitcast.72, bf16[640,256]{1,0:T(8,128)(2,1)} %get-tuple-element.113.embed_ref, ...), custom_call_target="tpu_custom_call" | custom-call | tf_op jit(solution)/shard_map/cond/branch_1_fun/pallas_call | solution.py:435
  102.0 0.7 copy.43

commit v3 on v2

--- a/solution.py
+++ b/solution.py
@@ -11,6 +11,7 @@
 MESH_ID = pl.DeviceIdType.MESH
 KEEP = 32
 HALF = KEEP // 2
+GROUP = 7
 REACH = 2
 OWN = 16
 NEAR_ROWS = 256
@@ -100,6 +101,18 @@
     return (own_cols.astype(jnp.float32) + decoded).astype(jnp.bfloat16)
 
 
+def torus(n):
+    wide = 1 << (n.bit_length() // 2)
+    return n // wide, wide
+
+
+def visit_order(n):
+    tall, wide = torus(n)
+    offsets = [(r, c) for r in range(tall) for c in range(wide)][1:]
+    offsets.sort(key=lambda o: min(o[0], tall - o[0]) + min(o[1], wide - o[1]))
+    return [offsets[i // 2] if i % 2 == 0 else offsets[-1 - i // 2] for i in range(n - 1)]
+
+
 def silu(v):
     return v / (1.0 + jnp.exp(-v))
 
@@ -122,8 +135,8 @@
     n, hot_ref, grid_ref, wsrc_ref, bias_ref, embed_ref, wnode_ref, wdec_ref,
     src_ref, dst_ref, count_ref, out_ref,
     src_live, dst_live, srcx_ref, dstx_ref,
-    base_out, near_out, base_in, near_in, dst_in, emb_in, part_out, part_in,
-    acc, hid_out, hid_in, prj_out, prj_in, back_out, nback_out, back_in, nback_in, hot_out, hot_in, dec,
+    base_out, near_out, base_in, near_in, dst_in, emb_in, emb_out, emb_half, part_out, part_in,
+    acc, hid_out, hid_in, prj_out, prj_in, prj_bf, back_out, nback_out, back_in, nback_in, hot_out, hot_in, dec,
     ssem, rsem,
 ):
     me = lax.axis_index("graph")
@@ -153,7 +166,28 @@
             src_ref=src, dst_ref=dst, send_sem=ssem.at[k], recv_sem=rsem.at[k],
             device_id={"chan": other}, device_id_type=MESH_ID)
 
-    DST, EMB, BASE, NEAR, PART, FWDB, FWDN, HID, PRJ, BACK, NBACK, HOT = range(12)
+    tall, wide = torus(n)
+    codes = [r * wide + c for r, c in visit_order(n)]
+    groups = [codes[i:i + GROUP] for i in range(0, n - 1, GROUP)]
+    my_row, my_column = me // wide, lax.rem(me, wide)
+    turn = 1 - 2 * core
+
+    def each_peer(visit):
+        parts = (range(0, 4), range(4, GROUP))
+
+        @pl.loop(0, len(groups))
+        def _(g):
+            for part in parts:
+                packed = jnp.int32(0)
+                for i, group in enumerate(groups):
+                    packed = jnp.where(g == i, sum(group[k] * n ** j for j, k in enumerate(part)), packed)
+                for j in range(len(part)):
+                    code = lax.rem(lax.div(packed, jnp.int32(n ** j)), jnp.int32(n))
+                    to_row = lax.rem(my_row + turn * lax.div(code, jnp.int32(wide)) + tall, tall)
+                    to_column = lax.rem(my_column + turn * lax.rem(code, jnp.int32(wide)) + wide, wide)
+                    visit(to_row * wide + to_column)
+
+    DST, EMB, BASE, NEAR, PART, FWDB, FWDN, HID, PRJ, BACK, NBACK, HOT, PRJ0, BACK1 = range(14)
 
     blocks = (n * HALF) // CHUNK
     capacity = dst_ref.shape[2]
@@ -201,15 +235,8 @@
 
     pl.semaphore_wait(barrier, n)
 
-    @pl.loop(1, n)
-    def _(i):
-        peer = lax.rem(me + i, n)
-        to_graph(dst_ref.at[peer], dst_in.at[me], DST, peer).start()
-
-    @pl.loop(1, n)
-    def _(i):
-        peer = lax.rem(me + i, n)
-        to_graph(base_out.at[peer], base_in.at[core, me], BASE, peer).start()
+    each_peer(lambda peer: to_graph(dst_ref.at[peer], dst_in.at[me], DST, peer).start())
+    each_peer(lambda peer: to_graph(base_out.at[peer], base_in.at[core, me], BASE, peer).start())
 
     for o in range(-REACH, REACH + 1):
         rows = pl.ds((o + REACH) * span, span)
@@ -217,12 +244,6 @@
             near_in[core, (o + REACH) * span:(o + REACH + 1) * span] = near_out[(o + REACH) * span:(o + REACH + 1) * span]
         else:
             to_graph(near_out.at[rows], near_in.at[core, rows], NEAR, lax.rem(me + o + n, n)).start()
-
-    @pl.loop(0, owners)
-    def _(p):
-        @pl.when(p != me)
-        def _():
-            to_graph(embed_ref.at[pl.ds(p * OWN, OWN)], emb_in.at[me], EMB, p).start()
 
     base_in[core, pl.ds(me, 1)] = base_out[pl.ds(me, 1)]
     dst_in[pl.ds(me, 1)] = dst_ref[pl.ds(me, 1)]
@@ -235,11 +256,29 @@
     part = jnp.dot(spread(mesh_rows, hot_dst), msgs, preferred_element_type=jnp.float32).astype(bf)
     part_out[...] = part.reshape(owners, OWN, part.shape[1])
 
-    @pl.loop(0, owners)
-    def _(p):
-        @pl.when(p != me)
+    def send_part(peer):
+        @pl.when(peer < owners)
         def _():
-            to_graph(part_out.at[p], part_in.at[me], PART, p).start()
+            to_graph(part_out.at[peer], part_in.at[me], PART, peer).start()
+
+    each_peer(send_part)
+
+    quarter = prj_out.shape[1]
+    w_other = wdec_ref[:, pl.ds(pl.multiple_of(other * quarter, quarter), quarter)]
+    w_own = wdec_ref[:, pl.ds(pl.multiple_of(core * quarter, quarter), quarter)]
+    prj_out[0:mesh_rows] = jnp.dot(embed_ref[...], w_other, preferred_element_type=jnp.float32)
+    send0 = to_core(prj_out.at[pl.ds(0, mesh_rows)], emb_half, PRJ0)
+    send0.start()
+    emb_own = jnp.dot(embed_ref[...], w_own, preferred_element_type=jnp.float32)
+    send0.wait_recv()
+    emb_out[...] = (emb_own + emb_half[...]).astype(bf).reshape(owners, OWN, quarter)
+
+    def send_emb(peer):
+        @pl.when(peer < owners)
+        def _():
+            to_graph(emb_out.at[peer], emb_in.at[me], EMB, peer).start()
+
+    each_peer(send_emb)
 
     def wait_in(ref, k):
         to_graph(ref, ref, k, me).wait_recv()
@@ -272,7 +311,7 @@
         wait_in(part_in.at[pl.ds(0, n - 1)], PART)
         wait_in(emb_in.at[pl.ds(0, n - 1)], EMB)
         part_in[pl.ds(me, 1)] = part_out[pl.ds(me, 1)]
-        emb_in[pl.ds(me, 1)] = embed_ref[pl.ds(me * OWN, OWN)].reshape(1, OWN, embed_ref.shape[1])
+        emb_in[pl.ds(me, 1)] = emb_out[pl.ds(me, 1)]
         acc[mesh_rows:mesh_rows + OWN] = part_in[...].astype(jnp.float32).sum(axis=0)
 
     half = hid_out.shape[1]
@@ -283,11 +322,9 @@
     own = jnp.dot(agg, wnode_ref[:, pl.ds(pl.multiple_of(core * half, half), half)], preferred_element_type=jnp.float32)
     send.wait_recv()
     nodes = silu(own + hid_in[...])
-    quarter = prj_out.shape[1]
     lat = (embed_ref[...].astype(jnp.float32) + nodes[0:mesh_rows]).astype(bf)
-    hot_lat = (emb_in[hot].astype(jnp.float32) + nodes[mesh_rows:]).astype(bf)
-    w_other = wdec_ref[:, pl.ds(pl.multiple_of(other * quarter, quarter), quarter)]
-    w_own = wdec_ref[:, pl.ds(pl.multiple_of(core * quarter, quarter), quarter)]
+    hot_lat = nodes[mesh_rows:].astype(bf)
+    send0.wait_send()
     prj_out[0:mesh_rows] = jnp.dot(lat, w_other, preferred_element_type=jnp.float32)
     prj_out[mesh_rows:] = jnp.dot(hot_lat, w_other, preferred_element_type=jnp.float32)
     send2 = to_core(prj_out, prj_in, PRJ)
@@ -296,38 +333,32 @@
     own_h = jnp.dot(hot_lat, w_own, preferred_element_type=jnp.float32)
     send2.wait_recv()
     proj = (own_p + prj_in[0:mesh_rows]).astype(bf)
-    hot_out[...] = (own_h + prj_in[mesh_rows:]).astype(bf)
+    hot_out[...] = (own_h + prj_in[mesh_rows:] + emb_in[hot].astype(jnp.float32)).astype(bf)
 
     @pl.when(me < owners)
     def _():
-        @pl.loop(1, n)
-        def _(i):
-            peer = lax.rem(me + i, n)
-            to_graph(hot_out, hot_in.at[me], HOT, peer).start()
-
+        each_peer(lambda peer: to_graph(hot_out, hot_in.at[me], HOT, peer).start())
+
+    prj_bf[...] = proj
     for h in range(2):
-        @pl.loop(0, blocks)
-        def _(j):
-            idx = dstx_ref[h, pl.ds(j, 1)]
-            rows = pick_turned(proj, idx).T.astype(bf)
-            back_out[h, pl.ds(j * (CHUNK // HALF), CHUNK // HALF)] = rows.reshape(CHUNK // HALF, HALF, rows.shape[1])
-        nback_out[h] = pick_turned(proj, dstx_ref[h, blocks:]).T.astype(bf)
-
-    @pl.loop(1, n)
-    def _(i):
-        peer = lax.rem(me + i, n)
-        to_graph(back_out.at[:, peer], back_in.at[:, me], BACK, peer).start()
-
-    for h in range(2):
+        nback_out[h] = pick_turned(prj_bf[...], dstx_ref[h, blocks:]).T.astype(bf)
+        nback_in[h, used:, :] = jnp.zeros((NEAR_ROWS - used, nback_in.shape[2]), bf)
         for o in range(-REACH, REACH + 1):
             a = (o + REACH) * span
             if o == 0:
                 nback_in[h, a:a + span] = nback_out[h, a:a + span]
             else:
                 to_graph(nback_out.at[h, pl.ds(a, span)], nback_in.at[h, pl.ds(a, span)], NBACK, lax.rem(me - o + n, n)).start()
-        nback_in[h, used:, :] = jnp.zeros((NEAR_ROWS - used, nback_in.shape[2]), bf)
+
     for h in range(2):
+        @pl.loop(0, blocks)
+        def _(j):
+            idx = dstx_ref[h, pl.ds(j, 1)]
+            rows = pick_turned(prj_bf[...], idx).T.astype(bf)
+            back_out[h, pl.ds(j * (CHUNK // HALF), CHUNK // HALF)] = rows.reshape(CHUNK // HALF, HALF, rows.shape[1])
+
         back_in[h, pl.ds(me, 1)] = back_out[h, pl.ds(me, 1)]
+        each_peer(lambda peer, h=h: to_graph(back_out.at[h, peer], back_in.at[h, me], BACK1 if h else BACK, peer).start())
 
     dec[...] = grid_ref[:, pl.ds(pl.multiple_of(core * quarter, quarter), quarter)].astype(jnp.float32)
     wait_in(nback_in.at[:, pl.ds(0, 2 * REACH * span)], NBACK)
@@ -346,8 +377,9 @@
     hot_rows = pick_turned(hot_in[...].reshape(mesh_rows, quarter), hot_dst).astype(bf)
     dec[...] += lax.dot_general(spread(grid_rows, hot_src), hot_rows, (((1,), (1,)), ((), ())), preferred_element_type=jnp.float32)
 
-    wait_in(back_in.at[:, pl.ds(0, n - 1)], BACK)
     for h in range(2):
+        wait_in(back_in.at[h, pl.ds(0, n - 1)], BACK1 if h else BACK)
+
         @pl.loop(0, blocks)
         def _(j):
             rows = back_in[h, pl.ds(j * (CHUNK // HALF), CHUNK // HALF)].reshape(CHUNK, quarter)
@@ -365,20 +397,21 @@
 
     @pl.when(me < owners)
     def _():
-        wait_out(embed_ref.at[pl.ds(0, mesh_rows - OWN)], EMB)
+        wait_out(emb_out.at[pl.ds(0, owners - 1)], EMB)
         wait_out(part_out.at[pl.ds(0, owners - 1)], PART)
         wait_out(back_out.at[0, pl.ds(0, n - 1)], HOT)
 
     @pl.when(me >= owners)
     def _():
-        wait_out(embed_ref, EMB)
+        wait_out(emb_out, EMB)
         wait_out(part_out, PART)
 
     to_core(base_in.at[core], base_in.at[core], FWDB).wait_send()
     to_core(near_in.at[core], near_in.at[core], FWDN).wait_send()
     send.wait_send()
     send2.wait_send()
-    wait_out(back_out.at[:, pl.ds(0, n - 1)], BACK)
+    for h in range(2):
+        wait_out(back_out.at[h, pl.ds(0, n - 1)], BACK1 if h else BACK)
     wait_out(nback_out.at[:, pl.ds(0, 2 * REACH * span)], NBACK)
 
 
@@ -442,16 +475,16 @@
             vm((2, n * HALF // CHUNK + 1, CHUNK), jnp.int32), vm((2, n * HALF // CHUNK + 1, CHUNK), jnp.int32),
             vm((n, HALF, width), bf), vm((NEAR_ROWS, width), bf),
             vm((2, n, HALF, width), bf), vm((2, NEAR_ROWS, width), bf),
-            vm((n, 1, capacity), jnp.int32), vm((n, OWN, half), bf),
+            vm((n, 1, capacity), jnp.int32), vm((n, OWN, quarter), bf), vm((owners, OWN, quarter), bf), vm((mesh_rows, quarter), f32),
             vm((owners, OWN, half), bf), vm((n, OWN, half), bf),
             vm((mesh_rows + OWN, half), f32),
             vm((mesh_rows + OWN, half), f32), vm((mesh_rows + OWN, half), f32),
-            vm((mesh_rows + OWN, quarter), f32), vm((mesh_rows + OWN, quarter), f32),
+            vm((mesh_rows + OWN, quarter), f32), vm((mesh_rows + OWN, quarter), f32), vm((mesh_rows, quarter), bf),
             vm((2, n, HALF, quarter), bf), vm((2, NEAR_ROWS, quarter), bf),
             vm((2, n, HALF, quarter), bf), vm((2, NEAR_ROWS, quarter), bf),
             vm((OWN, quarter), bf), vm((owners, OWN, quarter), bf),
             vm((grid_rows, quarter), f32),
-            pltpu.SemaphoreType.DMA((12,)), pltpu.SemaphoreType.DMA((12,)),
+            pltpu.SemaphoreType.DMA((14,)), pltpu.SemaphoreType.DMA((14,)),
         ],
         compiler_params=pltpu.CompilerParams(collective_id=0, has_side_effects=True, vmem_limit_bytes=48 * 1024 * 1024),
     )(hot, grid_state, w_src, bias_src[None, :], mesh_embed, w_node, w_dec, slot_src, slot_dst, slot_count)

time: 105 us -> 95.4 us (0.909)
  the two profiles are of different devices: /device:TPU:640 before, /device:TPU:646 now
where the time goes in v3:
time: 95.4 us; the launch traced here: 95.2 us
  Pallas kernels  91.5 us (96%)
  other arithmetic  1.49 us (2%)
  between operations  1.3 us (1%)
    pallas_call x1, Pallas kernels, compact(): pl.pallas_call(functools.partial(step_kernel, n), out_shape=jax.ShapeDtyp...  91.5 us

profile of v3, /device:TPU:646, one launch (start us, length us, event | category | flops | bytes accessed | tf_op | source)
XLA Modules:
  0.0 95.2 jit_solution(16056497145857141784)
XLA Ops:
  0.0 1.5 %select_reduce_fusion = (s32[]{:T(128)}, s32[]{:T(128)}) fusion(s32[64,64]{1,0:T(8,128)} %param.23), kind=kLoop, calls=%fused_computation.52 | loop fusion | flops 45054 | bytes 16392 | tf_op jit(solution)/shard_map/reduce_min | solution.py:501
  2.8 91.7 %conditional.1 = (bf16[1024,128]{1,0:T(8,128)(2,1)S(1)}) conditional(s32[]{:T(128)} %convert_element_type.26, (bf16[1024,256]{1,0:T(8,128)(2,1)}, s32[64,64]{1,0:T(8,128)}, s32[1,64,128]{2,1,0:T(8,128)}, s32[64,1,128]{2,1,0:T(1,128)}, bf16[640,256]{1,0:T(8,128)(2,1)}, /*index=5*/bf16[256,256]{1,0:T(8,128)(2,1)}, f32[256]{0:T(256)}, ...), branch_computations={%region_2.9_spmd, %region_9.10_spmd} | conditional | flops 2573017088 | bytes 80659304 | solution.py:504
  3.0 91.5 %branch_1_fun.1 = bf16[1024,128]{1,0:T(8,128)(2,1)S(1)} custom-call(s32[1]{0:T(128)} %bitcast.17.hot_ref, bf16[1024,256]{1,0:T(8,128)(2,1)} %get-tuple-element.110.grid_ref, bf16[256,256]{1,0:T(8,128)(2,1)} %get-tuple-element.111.wsrc_ref, f32[1,256]{1,0:T(1,128)} %bitcast.72, bf16[640,256]{1,0:T(8,128)(2,1)} %get-tuple-element.113.embed_ref, ...), custom_call_target="tpu_custom_call" | custom-call | tf_op jit(solution)/shard_map/cond/branch_1_fun/pallas_call | solution.py:468
  94.5 0.7 copy.43

commit v4 on v3

--- a/solution.py
+++ b/solution.py
@@ -12,6 +12,7 @@
 KEEP = 32
 HALF = KEEP // 2
 GROUP = 7
+SEMS = 16
 REACH = 2
 OWN = 16
 NEAR_ROWS = 256
@@ -114,7 +115,8 @@
 
 
 def silu(v):
-    return v / (1.0 + jnp.exp(-v))
+    h = 0.5 * v
+    return h + h * jnp.tanh(h)
 
 
 def pick_turned(table, idx):
@@ -132,12 +134,13 @@
 
 
 def step_kernel(
-    n, hot_ref, grid_ref, wsrc_ref, bias_ref, embed_ref, wnode_ref, wdec_ref,
-    src_ref, dst_ref, count_ref, out_ref,
+    n, hot_ref, grid_hbm, wsrc_hbm, bias_hbm, embed_hbm, wnode_hbm, wdec_hbm, src_hbm, dst_hbm, count_hbm, out_ref,
+    grid_ref, wsrc_ref, bias_ref, embed_ref, wnode_ref, wdec_ref, src_ref, dst_ref, count_ref,
     src_live, dst_live, srcx_ref, dstx_ref,
     base_out, near_out, base_in, near_in, dst_in, emb_in, emb_out, emb_half, part_out, part_in,
     acc, hid_out, hid_in, prj_out, prj_in, prj_bf, back_out, nback_out, back_in, nback_in, hot_out, hot_in, dec,
-    ssem, rsem,
+    hhid_out, hhid_in, hprj_out, hprj_in,
+    lsem, ssem, rsem,
 ):
     me = lax.axis_index("graph")
     core = lax.axis_index("chan")
@@ -146,14 +149,41 @@
     mesh_rows = embed_ref.shape[0]
     owners = mesh_rows // OWN
     span = cap_near(dst_ref.shape[2])
+    used = (2 * REACH + 1) * span
+    half = hid_out.shape[1]
+    quarter = prj_out.shape[1]
     bf = jnp.bfloat16
+    dot = functools.partial(jnp.dot, preferred_element_type=jnp.float32)
+
+    pairs = (
+        (src_hbm, src_ref), (dst_hbm, dst_ref), (count_hbm, count_ref), (grid_hbm, grid_ref), (embed_hbm, embed_ref),
+        (wdec_hbm, wdec_ref), (wsrc_hbm, wsrc_ref), (bias_hbm, bias_ref), (wnode_hbm, wnode_ref),
+    )
+    SRC, DSTS, COUNT, GRID, EMBED, WDEC, WSRC, BIAS, WNODE = (
+        pltpu.make_async_copy(x, y, lsem.at[i]) for i, (x, y) in enumerate(pairs))
+    for copy in (SRC, DSTS, COUNT, GRID, EMBED, WDEC, WSRC, BIAS, WNODE):
+        copy.start()
+
+    tall, wide = torus(n)
+    codes = [r * 2 * wide + c for r, c in visit_order(n)]
+    groups = [codes[i:i + GROUP] for i in range(0, n - 1, GROUP)]
+    spot = 2 * wide * (me // wide) + lax.rem(me, wide) + core * (2 * wide * tall + wide)
+    turn = 1 - 2 * core
+
+    def each_peer(visit):
+        @pl.loop(0, len(groups))
+        def _(g):
+            for part in (range(0, 4), range(4, GROUP)):
+                packed = jnp.int32(0)
+                for i, group in enumerate(groups):
+                    packed = jnp.where(g == i, sum(group[k] << (7 * j) for j, k in enumerate(part)), packed)
+                for j in range(len(part)):
+                    code = lax.shift_right_logical(packed, jnp.int32(7 * j)) & 127
+                    at = spot + turn * code
+                    visit((lax.shift_right_logical(at, jnp.int32(1)) & ((tall - 1) * wide)) + (at & (wide - 1)))
 
     barrier = pltpu.get_barrier_semaphore()
-
-    @pl.loop(1, n)
-    def _(i):
-        pl.semaphore_signal(barrier, inc=1, device_id={"graph": lax.rem(me + i, n)}, device_id_type=MESH_ID)
-
+    each_peer(lambda peer: pl.semaphore_signal(barrier, inc=1, device_id={"graph": peer}, device_id_type=MESH_ID))
     pl.semaphore_signal(barrier, inc=1, device_id={"chan": other}, device_id_type=MESH_ID)
 
     def to_graph(src, dst, k, peer):
@@ -166,31 +196,19 @@
             src_ref=src, dst_ref=dst, send_sem=ssem.at[k], recv_sem=rsem.at[k],
             device_id={"chan": other}, device_id_type=MESH_ID)
 
-    tall, wide = torus(n)
-    codes = [r * wide + c for r, c in visit_order(n)]
-    groups = [codes[i:i + GROUP] for i in range(0, n - 1, GROUP)]
-    my_row, my_column = me // wide, lax.rem(me, wide)
-    turn = 1 - 2 * core
-
-    def each_peer(visit):
-        parts = (range(0, 4), range(4, GROUP))
-
-        @pl.loop(0, len(groups))
-        def _(g):
-            for part in parts:
-                packed = jnp.int32(0)
-                for i, group in enumerate(groups):
-                    packed = jnp.where(g == i, sum(group[k] * n ** j for j, k in enumerate(part)), packed)
-                for j in range(len(part)):
-                    code = lax.rem(lax.div(packed, jnp.int32(n ** j)), jnp.int32(n))
-                    to_row = lax.rem(my_row + turn * lax.div(code, jnp.int32(wide)) + tall, tall)
-                    to_column = lax.rem(my_column + turn * lax.rem(code, jnp.int32(wide)) + wide, wide)
-                    visit(to_row * wide + to_column)
-
-    DST, EMB, BASE, NEAR, PART, FWDB, FWDN, HID, PRJ, BACK, NBACK, HOT, PRJ0, BACK1 = range(14)
+    def wait_in(ref, k):
+        to_graph(ref, ref, k, me).wait_recv()
+
+    def wait_out(ref, k):
+        to_graph(ref, ref, k, me).wait_send()
+
+    DST, EMB, BASE, NEAR, PART, FWDB, FWDN, HID, PRJ, BACK, NBACK, HOT, PRJ0, BACK1, HIDH, PRJH = range(SEMS)
 
     blocks = (n * HALF) // CHUNK
     capacity = dst_ref.shape[2]
+    SRC.wait()
+    DSTS.wait()
+    COUNT.wait()
     with jax.named_scope("index"):
         hot = hot_ref[0]
         ids = lax.broadcasted_iota(jnp.int32, (n, n), 0)
@@ -223,76 +241,64 @@
             srcx_ref[h, blocks:] = lay_out(near_src, *near)[:, 0:CHUNK]
             dstx_ref[h, blocks:] = lay_out(near_dst, *near)[:, 0:CHUNK]
 
+    GRID.wait()
+
     @pl.loop(0, blocks)
     def _(j):
-        idx = srcx_ref[core, pl.ds(j, 1)]
-        rows = pick_turned(grid_ref[...], idx).T.astype(bf)
+        rows = pick_turned(grid_ref[...], srcx_ref[core, pl.ds(j, 1)]).T.astype(bf)
         base_out[pl.ds(j * (CHUNK // HALF), CHUNK // HALF)] = rows.reshape(CHUNK // HALF, HALF, rows.shape[1])
 
     near_out[...] = pick_turned(grid_ref[...], srcx_ref[core, blocks:]).T.astype(bf)
-    used = (2 * REACH + 1) * span
     near_in[core, used:, :] = jnp.zeros((NEAR_ROWS - used, near_in.shape[2]), bf)
 
     pl.semaphore_wait(barrier, n)
-
     each_peer(lambda peer: to_graph(dst_ref.at[peer], dst_in.at[me], DST, peer).start())
-    each_peer(lambda peer: to_graph(base_out.at[peer], base_in.at[core, me], BASE, peer).start())
-
     for o in range(-REACH, REACH + 1):
         rows = pl.ds((o + REACH) * span, span)
         if o == 0:
             near_in[core, (o + REACH) * span:(o + REACH + 1) * span] = near_out[(o + REACH) * span:(o + REACH + 1) * span]
         else:
             to_graph(near_out.at[rows], near_in.at[core, rows], NEAR, lax.rem(me + o + n, n)).start()
-
+    each_peer(lambda peer: to_graph(base_out.at[peer], base_in.at[core, me], BASE, peer).start())
     base_in[core, pl.ds(me, 1)] = base_out[pl.ds(me, 1)]
     dst_in[pl.ds(me, 1)] = dst_ref[pl.ds(me, 1)]
 
-    to_graph(dst_ref.at[pl.ds(0, n - 1)], dst_in.at[pl.ds(0, n - 1)], DST, me).wait_recv()
+    EMBED.wait()
+    WDEC.wait()
+    w_other = wdec_ref[:, pl.ds(pl.multiple_of(other * quarter, quarter), quarter)]
+    w_own = wdec_ref[:, pl.ds(pl.multiple_of(core * quarter, quarter), quarter)]
+    prj_out[...] = dot(embed_ref[...], w_other)
+    send0 = to_core(prj_out, emb_half, PRJ0)
+    send0.start()
+    WSRC.wait()
+    BIAS.wait()
     hot_src = src_live[pl.ds(hot, 1)].astype(jnp.int32) - 1
+    msgs = silu(dot(pick_turned(grid_ref[...], hot_src).T.astype(bf), wsrc_ref[...]) + bias_ref[...]).astype(bf)
+    emb_own = dot(embed_ref[...], w_own)
+    send0.wait_recv()
+    emb_out[...] = (emb_own + emb_half[...]).astype(bf).reshape(owners, OWN, quarter)
+
+    wait_in(dst_in.at[pl.ds(0, n - 1)], DST)
     hot_dst = jnp.where(hot_src >= 0, dst_in[hot], -1)
-    rows = pick_turned(grid_ref[...], hot_src).T.astype(bf)
-    msgs = silu(jnp.dot(rows, wsrc_ref[...], preferred_element_type=jnp.float32) + bias_ref[...]).astype(bf)
-    part = jnp.dot(spread(mesh_rows, hot_dst), msgs, preferred_element_type=jnp.float32).astype(bf)
-    part_out[...] = part.reshape(owners, OWN, part.shape[1])
-
-    def send_part(peer):
+    part_out[...] = dot(spread(mesh_rows, hot_dst), msgs).astype(bf).reshape(owners, OWN, half)
+
+    def send_share(peer):
         @pl.when(peer < owners)
         def _():
             to_graph(part_out.at[peer], part_in.at[me], PART, peer).start()
-
-    each_peer(send_part)
-
-    quarter = prj_out.shape[1]
-    w_other = wdec_ref[:, pl.ds(pl.multiple_of(other * quarter, quarter), quarter)]
-    w_own = wdec_ref[:, pl.ds(pl.multiple_of(core * quarter, quarter), quarter)]
-    prj_out[0:mesh_rows] = jnp.dot(embed_ref[...], w_other, preferred_element_type=jnp.float32)
-    send0 = to_core(prj_out.at[pl.ds(0, mesh_rows)], emb_half, PRJ0)
-    send0.start()
-    emb_own = jnp.dot(embed_ref[...], w_own, preferred_element_type=jnp.float32)
-    send0.wait_recv()
-    emb_out[...] = (emb_own + emb_half[...]).astype(bf).reshape(owners, OWN, quarter)
-
-    def send_emb(peer):
-        @pl.when(peer < owners)
-        def _():
             to_graph(emb_out.at[peer], emb_in.at[me], EMB, peer).start()
 
-    each_peer(send_emb)
-
-    def wait_in(ref, k):
-        to_graph(ref, ref, k, me).wait_recv()
+    each_peer(send_share)
 
     wait_in(base_in.at[core, pl.ds(0, n - 1)], BASE)
     to_core(base_in.at[core], base_in.at[core], FWDB).start()
     wait_in(near_in.at[core, pl.ds(0, 2 * REACH * span)], NEAR)
     to_core(near_in.at[core], near_in.at[core], FWDN).start()
-
     acc[...] = jnp.zeros_like(acc)
 
     def add_rows(rows, idx):
-        m = silu(jnp.dot(rows, wsrc_ref[...], preferred_element_type=jnp.float32) + bias_ref[...]).astype(bf)
-        acc[0:mesh_rows] += jnp.dot(spread(mesh_rows, idx), m, preferred_element_type=jnp.float32)
+        m = silu(dot(rows, wsrc_ref[...]) + bias_ref[...]).astype(bf)
+        acc[...] += dot(spread(mesh_rows, idx), m)
 
     def add_half(h):
         @pl.loop(0, blocks)
@@ -306,43 +312,40 @@
     to_core(near_in.at[other], near_in.at[other], FWDN).wait_recv()
     add_half(other)
 
+    WNODE.wait()
+    n_other = wnode_ref[:, pl.ds(pl.multiple_of(other * half, half), half)]
+    n_own = wnode_ref[:, pl.ds(pl.multiple_of(core * half, half), half)]
+    agg = acc[...].astype(bf)
+    hid_out[...] = dot(agg, n_other)
+    send = to_core(hid_out, hid_in, HID)
+    send.start()
+    own = dot(agg, n_own)
+    send0.wait_send()
+    send.wait_recv()
+    lat = (embed_ref[...].astype(jnp.float32) + silu(own + hid_in[...])).astype(bf)
+    prj_out[...] = dot(lat, w_other)
+    send2 = to_core(prj_out, prj_in, PRJ)
+    send2.start()
+    own_p = dot(lat, w_own)
+
     @pl.when(me < owners)
     def _():
         wait_in(part_in.at[pl.ds(0, n - 1)], PART)
         wait_in(emb_in.at[pl.ds(0, n - 1)], EMB)
         part_in[pl.ds(me, 1)] = part_out[pl.ds(me, 1)]
         emb_in[pl.ds(me, 1)] = emb_out[pl.ds(me, 1)]
-        acc[mesh_rows:mesh_rows + OWN] = part_in[...].astype(jnp.float32).sum(axis=0)
-
-    half = hid_out.shape[1]
-    agg = acc[...].astype(bf)
-    hid_out[...] = jnp.dot(agg, wnode_ref[:, pl.ds(pl.multiple_of(other * half, half), half)], preferred_element_type=jnp.float32)
-    send = to_core(hid_out, hid_in, HID)
-    send.start()
-    own = jnp.dot(agg, wnode_ref[:, pl.ds(pl.multiple_of(core * half, half), half)], preferred_element_type=jnp.float32)
-    send.wait_recv()
-    nodes = silu(own + hid_in[...])
-    lat = (embed_ref[...].astype(jnp.float32) + nodes[0:mesh_rows]).astype(bf)
-    hot_lat = nodes[mesh_rows:].astype(bf)
-    send0.wait_send()
-    prj_out[0:mesh_rows] = jnp.dot(lat, w_other, preferred_element_type=jnp.float32)
-    prj_out[mesh_rows:] = jnp.dot(hot_lat, w_other, preferred_element_type=jnp.float32)
-    send2 = to_core(prj_out, prj_in, PRJ)
-    send2.start()
-    own_p = jnp.dot(lat, w_own, preferred_element_type=jnp.float32)
-    own_h = jnp.dot(hot_lat, w_own, preferred_element_type=jnp.float32)
+
+    hot_agg = part_in[...].astype(jnp.float32).sum(axis=0).astype(bf)
+    hhid_out[...] = dot(hot_agg, n_other)
+    send3 = to_core(hhid_out, hhid_in, HIDH)
+    send3.start()
+    hot_own = dot(hot_agg, n_own)
+
     send2.wait_recv()
-    proj = (own_p + prj_in[0:mesh_rows]).astype(bf)
-    hot_out[...] = (own_h + prj_in[mesh_rows:] + emb_in[hot].astype(jnp.float32)).astype(bf)
-
-    @pl.when(me < owners)
-    def _():
-        each_peer(lambda peer: to_graph(hot_out, hot_in.at[me], HOT, peer).start())
-
-    prj_bf[...] = proj
+    prj_bf[...] = (own_p + prj_in[...]).astype(bf)
     for h in range(2):
         nback_out[h] = pick_turned(prj_bf[...], dstx_ref[h, blocks:]).T.astype(bf)
-        nback_in[h, used:, :] = jnp.zeros((NEAR_ROWS - used, nback_in.shape[2]), bf)
+        nback_in[h, used:, :] = jnp.zeros((NEAR_ROWS - used, quarter), bf)
         for o in range(-REACH, REACH + 1):
             a = (o + REACH) * span
             if o == 0:
@@ -350,20 +353,47 @@
             else:
                 to_graph(nback_out.at[h, pl.ds(a, span)], nback_in.at[h, pl.ds(a, span)], NBACK, lax.rem(me - o + n, n)).start()
 
-    for h in range(2):
+    def return_half(h):
         @pl.loop(0, blocks)
         def _(j):
-            idx = dstx_ref[h, pl.ds(j, 1)]
-            rows = pick_turned(prj_bf[...], idx).T.astype(bf)
-            back_out[h, pl.ds(j * (CHUNK // HALF), CHUNK // HALF)] = rows.reshape(CHUNK // HALF, HALF, rows.shape[1])
+            rows = pick_turned(prj_bf[...], dstx_ref[h, pl.ds(j, 1)]).T.astype(bf)
+            back_out[h, pl.ds(j * (CHUNK // HALF), CHUNK // HALF)] = rows.reshape(CHUNK // HALF, HALF, quarter)
 
         back_in[h, pl.ds(me, 1)] = back_out[h, pl.ds(me, 1)]
-        each_peer(lambda peer, h=h: to_graph(back_out.at[h, peer], back_in.at[h, me], BACK1 if h else BACK, peer).start())
+
+    return_half(0)
+    send3.wait_recv()
+    hot_lat = silu(hot_own + hhid_in[...]).astype(bf)
+    hprj_out[...] = dot(hot_lat, w_other)
+    send4 = to_core(hprj_out, hprj_in, PRJH)
+    send4.start()
+    hot_prj = dot(hot_lat, w_own) + emb_in[hot].astype(jnp.float32)
+    each_peer(lambda peer: to_graph(back_out.at[0, peer], back_in.at[0, me], BACK, peer).start())
+    return_half(1)
+    send4.wait_recv()
+    hot_out[...] = (hot_prj + hprj_in[...]).astype(bf)
+
+    def send_rest(peer):
+        to_graph(back_out.at[1, peer], back_in.at[1, me], BACK1, peer).start()
+
+        @pl.when(me < owners)
+        def _():
+            to_graph(hot_out, hot_in.at[me], HOT, peer).start()
+
+    each_peer(send_rest)
 
     dec[...] = grid_ref[:, pl.ds(pl.multiple_of(core * quarter, quarter), quarter)].astype(jnp.float32)
     wait_in(nback_in.at[:, pl.ds(0, 2 * REACH * span)], NBACK)
     for h in range(2):
-        dec[...] += jnp.dot(spread(grid_rows, srcx_ref[h, blocks:]), nback_in[h], preferred_element_type=jnp.float32)
+        dec[...] += dot(spread(grid_rows, srcx_ref[h, blocks:]), nback_in[h])
+
+    for h in range(2):
+        wait_in(back_in.at[h, pl.ds(0, n - 1)], BACK1 if h else BACK)
+
+        @pl.loop(0, blocks)
+        def _(j):
+            rows = back_in[h, pl.ds(j * (CHUNK // HALF), CHUNK // HALF)].reshape(CHUNK, quarter)
+            dec[...] += dot(spread(grid_rows, srcx_ref[h, pl.ds(j, 1)]), rows)
 
     @pl.when(me < owners)
     def _():
@@ -375,21 +405,8 @@
         wait_in(hot_in, HOT)
 
     hot_rows = pick_turned(hot_in[...].reshape(mesh_rows, quarter), hot_dst).astype(bf)
-    dec[...] += lax.dot_general(spread(grid_rows, hot_src), hot_rows, (((1,), (1,)), ((), ())), preferred_element_type=jnp.float32)
-
-    for h in range(2):
-        wait_in(back_in.at[h, pl.ds(0, n - 1)], BACK1 if h else BACK)
-
-        @pl.loop(0, blocks)
-        def _(j):
-            rows = back_in[h, pl.ds(j * (CHUNK // HALF), CHUNK // HALF)].reshape(CHUNK, quarter)
-            idx = srcx_ref[h, pl.ds(j, 1)]
-            dec[...] += jnp.dot(spread(grid_rows, idx), rows, preferred_element_type=jnp.float32)
-
-    out_ref[...] = dec[...].astype(bf)
-
-    def wait_out(ref, k):
-        to_graph(ref, ref, k, me).wait_send()
+    back = lax.dot_general(spread(grid_rows, hot_src), hot_rows, (((1,), (1,)), ((), ())), preferred_element_type=jnp.float32)
+    out_ref[...] = (dec[...] + back).astype(bf)
 
     wait_out(dst_ref.at[pl.ds(0, n - 1)], DST)
     wait_out(base_out.at[pl.ds(0, n - 1)], BASE)
@@ -408,8 +425,8 @@
 
     to_core(base_in.at[core], base_in.at[core], FWDB).wait_send()
     to_core(near_in.at[core], near_in.at[core], FWDN).wait_send()
-    send.wait_send()
-    send2.wait_send()
+    for copy in (send, send2, send3, send4):
+        copy.wait_send()
     for h in range(2):
         wait_out(back_out.at[h, pl.ds(0, n - 1)], BACK1 if h else BACK)
     wait_out(nback_out.at[:, pl.ds(0, 2 * REACH * span)], NBACK)
@@ -468,23 +485,26 @@
     return pl.pallas_call(
         functools.partial(step_kernel, n),
         out_shape=jax.ShapeDtypeStruct((grid_rows, quarter), bf),
-        in_specs=[pl.BlockSpec(memory_space=pltpu.SMEM)] + [pl.BlockSpec(memory_space=vm)] * 9,
+        in_specs=[pl.BlockSpec(memory_space=pltpu.SMEM)] + [pl.BlockSpec(memory_space=pl.ANY)] * 9,
         out_specs=pl.BlockSpec(memory_space=vm),
         scratch_shapes=[
+            vm((grid_rows, width), bf), vm(w_src.shape, bf), vm((1, half), f32), vm((mesh_rows, half), bf), vm(w_node.shape, bf),
+            vm(w_dec.shape, bf), vm(slot_src.shape, jnp.int32), vm(slot_dst.shape, jnp.int32), vm(slot_count.shape, jnp.int32),
             vm((n, capacity), f32), vm((n, capacity), f32),
             vm((2, n * HALF // CHUNK + 1, CHUNK), jnp.int32), vm((2, n * HALF // CHUNK + 1, CHUNK), jnp.int32),
             vm((n, HALF, width), bf), vm((NEAR_ROWS, width), bf),
             vm((2, n, HALF, width), bf), vm((2, NEAR_ROWS, width), bf),
             vm((n, 1, capacity), jnp.int32), vm((n, OWN, quarter), bf), vm((owners, OWN, quarter), bf), vm((mesh_rows, quarter), f32),
             vm((owners, OWN, half), bf), vm((n, OWN, half), bf),
-            vm((mesh_rows + OWN, half), f32),
-            vm((mesh_rows + OWN, half), f32), vm((mesh_rows + OWN, half), f32),
-            vm((mesh_rows + OWN, quarter), f32), vm((mesh_rows + OWN, quarter), f32), vm((mesh_rows, quarter), bf),
+            vm((mesh_rows, half), f32),
+            vm((mesh_rows, half), f32), vm((mesh_rows, half), f32),
+            vm((mesh_rows, quarter), f32), vm((mesh_rows, quarter), f32), vm((mesh_rows, quarter), bf),
             vm((2, n, HALF, quarter), bf), vm((2, NEAR_ROWS, quarter), bf),
             vm((2, n, HALF, quarter), bf), vm((2, NEAR_ROWS, quarter), bf),
             vm((OWN, quarter), bf), vm((owners, OWN, quarter), bf),
             vm((grid_rows, quarter), f32),
-            pltpu.SemaphoreType.DMA((14,)), pltpu.SemaphoreType.DMA((14,)),
+            vm((OWN, half), f32), vm((OWN, half), f32), vm((OWN, quarter), f32), vm((OWN, quarter), f32),
+            pltpu.SemaphoreType.DMA((9,)), pltpu.SemaphoreType.DMA((SEMS,)), pltpu.SemaphoreType.DMA((SEMS,)),
         ],
         compiler_params=pltpu.CompilerParams(collective_id=0, has_side_effects=True, vmem_limit_bytes=48 * 1024 * 1024),
     )(hot, grid_state, w_src, bias_src[None, :], mesh_embed, w_node, w_dec, slot_src, slot_dst, slot_count)

time: 95.4 us -> 87.5 us (0.917)
  the two profiles are of different devices: /device:TPU:646 before, /device:TPU:640 now
where the time goes in v4:
time: 87.5 us; the launch traced here: 87.3 us
  Pallas kernels  83.6 us (96%)
  other arithmetic  1.49 us (2%)
  between operations  1.3 us (1%)
    pallas_call x1, Pallas kernels, compact(): pl.pallas_call(functools.partial(step_kernel, n), out_shape=jax.ShapeDtyp...  83.6 us

profile of v4, /device:TPU:640, one launch (start us, length us, event | category | flops | bytes accessed | tf_op | source)
XLA Modules:
  0.0 87.3 jit_solution(9926752192842944606)
XLA Ops:
  0.0 1.5 %select_reduce_fusion = (s32[]{:T(128)}, s32[]{:T(128)}) fusion(s32[64,64]{1,0:T(8,128)} %param.23), kind=kLoop, calls=%fused_computation.52 | loop fusion | flops 45054 | bytes 16392 | tf_op jit(solution)/shard_map/reduce_min | solution.py:521
  2.8 83.8 %conditional.1 = (bf16[1024,128]{1,0:T(8,128)(2,1)S(1)}) conditional(s32[]{:T(128)} %convert_element_type.26, (bf16[1024,256]{1,0:T(8,128)(2,1)}, s32[64,64]{1,0:T(8,128)}, s32[1,64,128]{2,1,0:T(8,128)}, s32[64,1,128]{2,1,0:T(1,128)}, bf16[640,256]{1,0:T(8,128)(2,1)}, /*index=5*/bf16[256,256]{1,0:T(8,128)(2,1)}, f32[256]{0:T(256)}, ...), branch_computations={%region_2.9_spmd, %region_9.10_spmd} | conditional | flops 2573017088 | bytes 80659304 | solution.py:524
  3.0 83.6 %branch_1_fun.1 = bf16[1024,128]{1,0:T(8,128)(2,1)S(1)} custom-call(s32[1]{0:T(128)} %bitcast.17.hot_ref, bf16[1024,256]{1,0:T(8,128)(2,1)} %get-tuple-element.110.grid_hbm, bf16[256,256]{1,0:T(8,128)(2,1)} %get-tuple-element.111.wsrc_hbm, f32[1,256]{1,0:T(1,128)} %bitcast.72, bf16[640,256]{1,0:T(8,128)(2,1)} %get-tuple-element.113.embed_hbm, ...), custom_call_target="tpu_custom_call" | custom-call | tf_op jit(solution)/shard_map/cond/branch_1_fun/pallas_call | solution.py:485
  86.6 0.7 copy.43

commit v5 on v4

--- a/solution.py
+++ b/solution.py
@@ -243,10 +243,9 @@
 
     GRID.wait()
 
-    @pl.loop(0, blocks)
-    def _(j):
-        rows = pick_turned(grid_ref[...], srcx_ref[core, pl.ds(j, 1)]).T.astype(bf)
-        base_out[pl.ds(j * (CHUNK // HALF), CHUNK // HALF)] = rows.reshape(CHUNK // HALF, HALF, rows.shape[1])
+    for j in range(blocks):
+        rows = pick_turned(grid_ref[...], srcx_ref[core, j:j + 1]).T.astype(bf)
+        base_out[j * (CHUNK // HALF):(j + 1) * (CHUNK // HALF)] = rows.reshape(CHUNK // HALF, HALF, rows.shape[1])
 
     near_out[...] = pick_turned(grid_ref[...], srcx_ref[core, blocks:]).T.astype(bf)
     near_in[core, used:, :] = jnp.zeros((NEAR_ROWS - used, near_in.shape[2]), bf)
@@ -294,28 +293,25 @@
     to_core(base_in.at[core], base_in.at[core], FWDB).start()
     wait_in(near_in.at[core, pl.ds(0, 2 * REACH * span)], NEAR)
     to_core(near_in.at[core], near_in.at[core], FWDN).start()
-    acc[...] = jnp.zeros_like(acc)
-
-    def add_rows(rows, idx):
+    def share(rows, idx):
         m = silu(dot(rows, wsrc_ref[...]) + bias_ref[...]).astype(bf)
-        acc[...] += dot(spread(mesh_rows, idx), m)
-
-    def add_half(h):
-        @pl.loop(0, blocks)
-        def _(j):
-            rows = base_in[h, pl.ds(j * (CHUNK // HALF), CHUNK // HALF)].reshape(CHUNK, base_in.shape[3])
-            add_rows(rows, dstx_ref[h, pl.ds(j, 1)])
-        add_rows(near_in[h], dstx_ref[h, blocks:])
-
-    add_half(core)
+        return dot(spread(mesh_rows, idx), m)
+
+    def half_sum(h):
+        total = share(near_in[h], dstx_ref[h, blocks:])
+        for j in range(blocks):
+            rows = base_in[h, j * (CHUNK // HALF):(j + 1) * (CHUNK // HALF)].reshape(CHUNK, base_in.shape[3])
+            total = total + share(rows, dstx_ref[h, j:j + 1])
+        return total
+
+    acc[...] = half_sum(core)
     to_core(base_in.at[other], base_in.at[other], FWDB).wait_recv()
     to_core(near_in.at[other], near_in.at[other], FWDN).wait_recv()
-    add_half(other)
 
     WNODE.wait()
     n_other = wnode_ref[:, pl.ds(pl.multiple_of(other * half, half), half)]
     n_own = wnode_ref[:, pl.ds(pl.multiple_of(core * half, half), half)]
-    agg = acc[...].astype(bf)
+    agg = (acc[...] + half_sum(other)).astype(bf)
     hid_out[...] = dot(agg, n_other)
     send = to_core(hid_out, hid_in, HID)
     send.start()
@@ -328,19 +324,6 @@
     send2.start()
     own_p = dot(lat, w_own)
 
-    @pl.when(me < owners)
-    def _():
-        wait_in(part_in.at[pl.ds(0, n - 1)], PART)
-        wait_in(emb_in.at[pl.ds(0, n - 1)], EMB)
-        part_in[pl.ds(me, 1)] = part_out[pl.ds(me, 1)]
-        emb_in[pl.ds(me, 1)] = emb_out[pl.ds(me, 1)]
-
-    hot_agg = part_in[...].astype(jnp.float32).sum(axis=0).astype(bf)
-    hhid_out[...] = dot(hot_agg, n_other)
-    send3 = to_core(hhid_out, hhid_in, HIDH)
-    send3.start()
-    hot_own = dot(hot_agg, n_own)
-
     send2.wait_recv()
     prj_bf[...] = (own_p + prj_in[...]).astype(bf)
     for h in range(2):
@@ -353,47 +336,51 @@
             else:
                 to_graph(nback_out.at[h, pl.ds(a, span)], nback_in.at[h, pl.ds(a, span)], NBACK, lax.rem(me - o + n, n)).start()
 
-    def return_half(h):
-        @pl.loop(0, blocks)
-        def _(j):
-            rows = pick_turned(prj_bf[...], dstx_ref[h, pl.ds(j, 1)]).T.astype(bf)
-            back_out[h, pl.ds(j * (CHUNK // HALF), CHUNK // HALF)] = rows.reshape(CHUNK // HALF, HALF, quarter)
-
+    for h in range(2):
+        for j in range(blocks):
+            rows = pick_turned(prj_bf[...], dstx_ref[h, j:j + 1]).T.astype(bf)
+            back_out[h, j * (CHUNK // HALF):(j + 1) * (CHUNK // HALF)] = rows.reshape(CHUNK // HALF, HALF, quarter)
         back_in[h, pl.ds(me, 1)] = back_out[h, pl.ds(me, 1)]
-
-    return_half(0)
+        each_peer(lambda peer, h=h: to_graph(back_out.at[h, peer], back_in.at[h, me], BACK1 if h else BACK, peer).start())
+
+    @pl.when(me < owners)
+    def _():
+        wait_in(part_in.at[pl.ds(0, n - 1)], PART)
+        wait_in(emb_in.at[pl.ds(0, n - 1)], EMB)
+        part_in[pl.ds(me, 1)] = part_out[pl.ds(me, 1)]
+        emb_in[pl.ds(me, 1)] = emb_out[pl.ds(me, 1)]
+
+    hot_agg = part_in[...].astype(jnp.float32).sum(axis=0).astype(bf)
+    hhid_out[...] = dot(hot_agg, n_other)
+    send3 = to_core(hhid_out, hhid_in, HIDH)
+    send3.start()
+    hot_own = dot(hot_agg, n_own)
+
     send3.wait_recv()
     hot_lat = silu(hot_own + hhid_in[...]).astype(bf)
     hprj_out[...] = dot(hot_lat, w_other)
     send4 = to_core(hprj_out, hprj_in, PRJH)
     send4.start()
     hot_prj = dot(hot_lat, w_own) + emb_in[hot].astype(jnp.float32)
-    each_peer(lambda peer: to_graph(back_out.at[0, peer], back_in.at[0, me], BACK, peer).start())
-    return_half(1)
     send4.wait_recv()
     hot_out[...] = (hot_prj + hprj_in[...]).astype(bf)
 
-    def send_rest(peer):
-        to_graph(back_out.at[1, peer], back_in.at[1, me], BACK1, peer).start()
-
-        @pl.when(me < owners)
-        def _():
-            to_graph(hot_out, hot_in.at[me], HOT, peer).start()
-
-    each_peer(send_rest)
-
-    dec[...] = grid_ref[:, pl.ds(pl.multiple_of(core * quarter, quarter), quarter)].astype(jnp.float32)
+    @pl.when(me < owners)
+    def _():
+        each_peer(lambda peer: to_graph(hot_out, hot_in.at[me], HOT, peer).start())
+
     wait_in(nback_in.at[:, pl.ds(0, 2 * REACH * span)], NBACK)
+    total = grid_ref[:, pl.ds(pl.multiple_of(core * quarter, quarter), quarter)].astype(jnp.float32)
     for h in range(2):
-        dec[...] += dot(spread(grid_rows, srcx_ref[h, blocks:]), nback_in[h])
-
+        total = total + dot(spread(grid_rows, srcx_ref[h, blocks:]), nback_in[h])
+    dec[...] = total
     for h in range(2):
         wait_in(back_in.at[h, pl.ds(0, n - 1)], BACK1 if h else BACK)
-
-        @pl.loop(0, blocks)
-        def _(j):
-            rows = back_in[h, pl.ds(j * (CHUNK // HALF), CHUNK // HALF)].reshape(CHUNK, quarter)
-            dec[...] += dot(spread(grid_rows, srcx_ref[h, pl.ds(j, 1)]), rows)
+        total = dec[...]
+        for j in range(blocks):
+            rows = back_in[h, j * (CHUNK // HALF):(j + 1) * (CHUNK // HALF)].reshape(CHUNK, quarter)
+            total = total + dot(spread(grid_rows, srcx_ref[h, j:j + 1]), rows)
+        dec[...] = total
 
     @pl.when(me < owners)
     def _():

time: 87.5 us -> 81.3 us (0.929)
  Pallas kernels: 83.6 us -> 77.4 us
    pallas_call x1, Pallas kernels: 83.6 us -> 77.4 us  [compact(): pl.pallas_call(functools.partial(step_kernel, n), out_shape=jax.ShapeDtyp...]
where the time goes in v5:
time: 81.3 us; the launch traced here: 81.1 us
  Pallas kernels  77.4 us (95%)
  other arithmetic  1.49 us (2%)
  between operations  1.3 us (2%)
    pallas_call x1, Pallas kernels, compact(): pl.pallas_call(functools.partial(step_kernel, n), out_shape=jax.ShapeDtyp...  77.4 us

profile of v5, /device:TPU:640, one launch (start us, length us, event | category | flops | bytes accessed | tf_op | source)
XLA Modules:
  0.0 81.1 jit_solution(7680537389381704733)
XLA Ops:
  0.0 1.5 %select_reduce_fusion = (s32[]{:T(128)}, s32[]{:T(128)}) fusion(s32[64,64]{1,0:T(8,128)} %param.23), kind=kLoop, calls=%fused_computation.52 | loop fusion | flops 45054 | bytes 16392 | tf_op jit(solution)/shard_map/reduce_min | solution.py:508
  2.8 77.6 %conditional.1 = (bf16[1024,128]{1,0:T(8,128)(2,1)S(1)}) conditional(s32[]{:T(128)} %convert_element_type.26, (bf16[1024,256]{1,0:T(8,128)(2,1)}, s32[64,64]{1,0:T(8,128)}, s32[1,64,128]{2,1,0:T(8,128)}, s32[64,1,128]{2,1,0:T(1,128)}, bf16[640,256]{1,0:T(8,128)(2,1)}, /*index=5*/bf16[256,256]{1,0:T(8,128)(2,1)}, f32[256]{0:T(256)}, ...), branch_computations={%region_2.9_spmd, %region_9.10_spmd} | conditional | flops 2573017088 | bytes 80659304 | solution.py:511
  3.0 77.4 %branch_1_fun.1 = bf16[1024,128]{1,0:T(8,128)(2,1)S(1)} custom-call(s32[1]{0:T(128)} %bitcast.17.hot_ref, bf16[1024,256]{1,0:T(8,128)(2,1)} %get-tuple-element.110.grid_hbm, bf16[256,256]{1,0:T(8,128)(2,1)} %get-tuple-element.111.wsrc_hbm, f32[1,256]{1,0:T(1,128)} %bitcast.72, bf16[640,256]{1,0:T(8,128)(2,1)} %get-tuple-element.113.embed_hbm, ...), custom_call_target="tpu_custom_call" | custom-call | tf_op jit(solution)/shard_map/cond/branch_1_fun/pallas_call | solution.py:472
  80.4 0.7 copy.43

commit v6 on v5

--- a/solution.py
+++ b/solution.py
@@ -281,13 +281,15 @@
     hot_dst = jnp.where(hot_src >= 0, dst_in[hot], -1)
     part_out[...] = dot(spread(mesh_rows, hot_dst), msgs).astype(bf).reshape(owners, OWN, half)
 
-    def send_share(peer):
-        @pl.when(peer < owners)
-        def _():
-            to_graph(part_out.at[peer], part_in.at[me], PART, peer).start()
-            to_graph(emb_out.at[peer], emb_in.at[me], EMB, peer).start()
-
-    each_peer(send_share)
+    def to_owner(copy_to):
+        def visit(peer):
+            @pl.when(peer < owners)
+            def _():
+                copy_to(peer).start()
+        return visit
+
+    each_peer(to_owner(lambda peer: to_graph(part_out.at[peer], part_in.at[me], PART, peer)))
+    each_peer(to_owner(lambda peer: to_graph(emb_out.at[peer], emb_in.at[me], EMB, peer)))
 
     wait_in(base_in.at[core, pl.ds(0, n - 1)], BASE)
     to_core(base_in.at[core], base_in.at[core], FWDB).start()
@@ -341,14 +343,13 @@
             rows = pick_turned(prj_bf[...], dstx_ref[h, j:j + 1]).T.astype(bf)
             back_out[h, j * (CHUNK // HALF):(j + 1) * (CHUNK // HALF)] = rows.reshape(CHUNK // HALF, HALF, quarter)
         back_in[h, pl.ds(me, 1)] = back_out[h, pl.ds(me, 1)]
-        each_peer(lambda peer, h=h: to_graph(back_out.at[h, peer], back_in.at[h, me], BACK1 if h else BACK, peer).start())
+        if h == 0:
+            each_peer(lambda peer: to_graph(back_out.at[0, peer], back_in.at[0, me], BACK, peer).start())
 
     @pl.when(me < owners)
     def _():
         wait_in(part_in.at[pl.ds(0, n - 1)], PART)
-        wait_in(emb_in.at[pl.ds(0, n - 1)], EMB)
         part_in[pl.ds(me, 1)] = part_out[pl.ds(me, 1)]
-        emb_in[pl.ds(me, 1)] = emb_out[pl.ds(me, 1)]
 
     hot_agg = part_in[...].astype(jnp.float32).sum(axis=0).astype(bf)
     hhid_out[...] = dot(hot_agg, n_other)
@@ -361,13 +362,24 @@
     hprj_out[...] = dot(hot_lat, w_other)
     send4 = to_core(hprj_out, hprj_in, PRJH)
     send4.start()
-    hot_prj = dot(hot_lat, w_own) + emb_in[hot].astype(jnp.float32)
-    send4.wait_recv()
-    hot_out[...] = (hot_prj + hprj_in[...]).astype(bf)
+    hot_prj = dot(hot_lat, w_own)
 
     @pl.when(me < owners)
     def _():
-        each_peer(lambda peer: to_graph(hot_out, hot_in.at[me], HOT, peer).start())
+        wait_in(emb_in.at[pl.ds(0, n - 1)], EMB)
+        emb_in[pl.ds(me, 1)] = emb_out[pl.ds(me, 1)]
+
+    send4.wait_recv()
+    hot_out[...] = (hot_prj + hprj_in[...] + emb_in[hot].astype(jnp.float32)).astype(bf)
+
+    def send_rest(peer):
+        @pl.when(me < owners)
+        def _():
+            to_graph(hot_out, hot_in.at[me], HOT, peer).start()
+
+        to_graph(back_out.at[1, peer], back_in.at[1, me], BACK1, peer).start()
+
+    each_peer(send_rest)
 
     wait_in(nback_in.at[:, pl.ds(0, 2 * REACH * span)], NBACK)
     total = grid_ref[:, pl.ds(pl.multiple_of(core * quarter, quarter), quarter)].astype(jnp.float32)

time: 81.3 us -> 87.1 us (1.071)
  Pallas kernels: 77.4 us -> 83.2 us
    pallas_call x1, Pallas kernels: 77.4 us -> 83.2 us  [compact(): pl.pallas_call(functools.partial(step_kernel, n), out_shape=jax.ShapeDtyp...]
where the time goes in v6:
time: 87.1 us; the launch traced here: 86.9 us
  Pallas kernels  83.2 us (96%)
  other arithmetic  1.49 us (2%)
  between operations  1.3 us (1%)
    pallas_call x1, Pallas kernels, compact(): pl.pallas_call(functools.partial(step_kernel, n), out_shape=jax.ShapeDtyp...  83.2 us

profile of v6, /device:TPU:640, one launch (start us, length us, event | category | flops | bytes accessed | tf_op | source)
XLA Modules:
  0.0 86.9 jit_solution(14944295704330959118)
XLA Ops:
  0.0 1.5 %select_reduce_fusion = (s32[]{:T(128)}, s32[]{:T(128)}) fusion(s32[64,64]{1,0:T(8,128)} %param.23), kind=kLoop, calls=%fused_computation.52 | loop fusion | flops 45054 | bytes 16392 | tf_op jit(solution)/shard_map/reduce_min | solution.py:520
  2.8 83.4 %conditional.1 = (bf16[1024,128]{1,0:T(8,128)(2,1)S(1)}) conditional(s32[]{:T(128)} %convert_element_type.26, (bf16[1024,256]{1,0:T(8,128)(2,1)}, s32[64,64]{1,0:T(8,128)}, s32[1,64,128]{2,1,0:T(8,128)}, s32[64,1,128]{2,1,0:T(1,128)}, bf16[640,256]{1,0:T(8,128)(2,1)}, /*index=5*/bf16[256,256]{1,0:T(8,128)(2,1)}, f32[256]{0:T(256)}, ...), branch_computations={%region_2.9_spmd, %region_9.10_spmd} | conditional | flops 2573017088 | bytes 80659304 | solution.py:523
  3.0 83.2 %branch_1_fun.1 = bf16[1024,128]{1,0:T(8,128)(2,1)S(1)} custom-call(s32[1]{0:T(128)} %bitcast.17.hot_ref, bf16[1024,256]{1,0:T(8,128)(2,1)} %get-tuple-element.110.grid_hbm, bf16[256,256]{1,0:T(8,128)(2,1)} %get-tuple-element.111.wsrc_hbm, f32[1,256]{1,0:T(1,128)} %bitcast.72, bf16[640,256]{1,0:T(8,128)(2,1)} %get-tuple-element.113.embed_hbm, ...), custom_call_target="tpu_custom_call" | custom-call | tf_op jit(solution)/shard_map/cond/branch_1_fun/pallas_call | solution.py:484
  86.2 0.7 copy.43

commit v7 on v6

--- a/solution.py
+++ b/solution.py
@@ -182,6 +182,14 @@
                     at = spot + turn * code
                     visit((lax.shift_right_logical(at, jnp.int32(1)) & ((tall - 1) * wide)) + (at & (wide - 1)))
 
+    per_row = owners // tall
+
+    def seat(shard):
+        r = lax.shift_right_logical(shard, jnp.int32(wide.bit_length() - 1))
+        rank = (shard + 3 * r) & (wide - 1)
+        return rank < per_row, r * per_row + rank
+
+    mine, my_block = seat(me)
     barrier = pltpu.get_barrier_semaphore()
     each_peer(lambda peer: pl.semaphore_signal(barrier, inc=1, device_id={"graph": peer}, device_id_type=MESH_ID))
     pl.semaphore_signal(barrier, inc=1, device_id={"chan": other}, device_id_type=MESH_ID)
@@ -283,13 +291,15 @@
 
     def to_owner(copy_to):
         def visit(peer):
-            @pl.when(peer < owners)
+            owns, block = seat(peer)
+
+            @pl.when(owns)
             def _():
-                copy_to(peer).start()
+                copy_to(peer, block).start()
         return visit
 
-    each_peer(to_owner(lambda peer: to_graph(part_out.at[peer], part_in.at[me], PART, peer)))
-    each_peer(to_owner(lambda peer: to_graph(emb_out.at[peer], emb_in.at[me], EMB, peer)))
+    each_peer(to_owner(lambda peer, block: to_graph(part_out.at[block], part_in.at[me], PART, peer)))
+    each_peer(to_owner(lambda peer, block: to_graph(emb_out.at[block], emb_in.at[me], EMB, peer)))
 
     wait_in(base_in.at[core, pl.ds(0, n - 1)], BASE)
     to_core(base_in.at[core], base_in.at[core], FWDB).start()
@@ -343,13 +353,12 @@
             rows = pick_turned(prj_bf[...], dstx_ref[h, j:j + 1]).T.astype(bf)
             back_out[h, j * (CHUNK // HALF):(j + 1) * (CHUNK // HALF)] = rows.reshape(CHUNK // HALF, HALF, quarter)
         back_in[h, pl.ds(me, 1)] = back_out[h, pl.ds(me, 1)]
-        if h == 0:
-            each_peer(lambda peer: to_graph(back_out.at[0, peer], back_in.at[0, me], BACK, peer).start())
-
-    @pl.when(me < owners)
+        each_peer(lambda peer, h=h: to_graph(back_out.at[h, peer], back_in.at[h, me], BACK1 if h else BACK, peer).start())
+
+    @pl.when(mine)
     def _():
         wait_in(part_in.at[pl.ds(0, n - 1)], PART)
-        part_in[pl.ds(me, 1)] = part_out[pl.ds(me, 1)]
+        part_in[pl.ds(me, 1)] = part_out[pl.ds(my_block, 1)]
 
     hot_agg = part_in[...].astype(jnp.float32).sum(axis=0).astype(bf)
     hhid_out[...] = dot(hot_agg, n_other)
@@ -364,22 +373,17 @@
     send4.start()
     hot_prj = dot(hot_lat, w_own)
 
-    @pl.when(me < owners)
+    @pl.when(mine)
     def _():
         wait_in(emb_in.at[pl.ds(0, n - 1)], EMB)
-        emb_in[pl.ds(me, 1)] = emb_out[pl.ds(me, 1)]
+        emb_in[pl.ds(me, 1)] = emb_out[pl.ds(my_block, 1)]
 
     send4.wait_recv()
     hot_out[...] = (hot_prj + hprj_in[...] + emb_in[hot].astype(jnp.float32)).astype(bf)
 
-    def send_rest(peer):
-        @pl.when(me < owners)
-        def _():
-            to_graph(hot_out, hot_in.at[me], HOT, peer).start()
-
-        to_graph(back_out.at[1, peer], back_in.at[1, me], BACK1, peer).start()
-
-    each_peer(send_rest)
+    @pl.when(mine)
+    def _():
+        each_peer(lambda peer: to_graph(hot_out, hot_in.at[my_block], HOT, peer).start())
 
     wait_in(nback_in.at[:, pl.ds(0, 2 * REACH * span)], NBACK)
     total = grid_ref[:, pl.ds(pl.multiple_of(core * quarter, quarter), quarter)].astype(jnp.float32)
@@ -394,12 +398,12 @@
             total = total + dot(spread(grid_rows, srcx_ref[h, j:j + 1]), rows)
         dec[...] = total
 
-    @pl.when(me < owners)
+    @pl.when(mine)
     def _():
         wait_in(hot_in.at[pl.ds(0, owners - 1)], HOT)
-        hot_in[pl.ds(me, 1)] = hot_out[...].reshape(1, OWN, quarter)
-
-    @pl.when(me >= owners)
+        hot_in[pl.ds(my_block, 1)] = hot_out[...].reshape(1, OWN, quarter)
+
+    @pl.when(jnp.logical_not(mine))
     def _():
         wait_in(hot_in, HOT)
 
@@ -411,13 +415,13 @@
     wait_out(base_out.at[pl.ds(0, n - 1)], BASE)
     wait_out(near_out.at[pl.ds(0, 2 * REACH * span)], NEAR)
 
-    @pl.when(me < owners)
+    @pl.when(mine)
     def _():
         wait_out(emb_out.at[pl.ds(0, owners - 1)], EMB)
         wait_out(part_out.at[pl.ds(0, owners - 1)], PART)
         wait_out(back_out.at[0, pl.ds(0, n - 1)], HOT)
 
-    @pl.when(me >= owners)
+    @pl.when(jnp.logical_not(mine))
     def _():
         wait_out(emb_out, EMB)
         wait_out(part_out, PART)

time: 87.1 us -> 78.7 us (0.904)
  the two profiles are of different devices: /device:TPU:640 before, /device:TPU:513 now
where the time goes in v7:
time: 78.7 us; the launch traced here: 78.5 us
  Pallas kernels  74.8 us (95%)
  other arithmetic  1.49 us (2%)
  between operations  1.3 us (2%)
    pallas_call x1, Pallas kernels, compact(): pl.pallas_call(functools.partial(step_kernel, n), out_shape=jax.ShapeDtyp...  74.8 us

profile of v7, /device:TPU:513, one launch (start us, length us, event | category | flops | bytes accessed | tf_op | source)
XLA Modules:
  0.0 78.5 jit_solution(4395113314922585042)
XLA Ops:
  0.0 1.5 %select_reduce_fusion = (s32[]{:T(128)}, s32[]{:T(128)}) fusion(s32[64,64]{1,0:T(8,128)} %param.23), kind=kLoop, calls=%fused_computation.52 | loop fusion | flops 45054 | bytes 16392 | tf_op jit(solution)/shard_map/reduce_min | solution.py:524
  2.8 75.0 %conditional.1 = (bf16[1024,128]{1,0:T(8,128)(2,1)S(1)}) conditional(s32[]{:T(128)} %convert_element_type.26, (bf16[1024,256]{1,0:T(8,128)(2,1)}, s32[64,64]{1,0:T(8,128)}, s32[1,64,128]{2,1,0:T(8,128)}, s32[64,1,128]{2,1,0:T(1,128)}, bf16[640,256]{1,0:T(8,128)(2,1)}, /*index=5*/bf16[256,256]{1,0:T(8,128)(2,1)}, f32[256]{0:T(256)}, ...), branch_computations={%region_2.9_spmd, %region_9.10_spmd} | conditional | flops 2573017088 | bytes 80659304 | solution.py:527
  3.0 74.8 %branch_1_fun.1 = bf16[1024,128]{1,0:T(8,128)(2,1)S(1)} custom-call(s32[1]{0:T(128)} %bitcast.17.hot_ref, bf16[1024,256]{1,0:T(8,128)(2,1)} %get-tuple-element.110.grid_hbm, bf16[256,256]{1,0:T(8,128)(2,1)} %get-tuple-element.111.wsrc_hbm, f32[1,256]{1,0:T(1,128)} %bitcast.72, bf16[640,256]{1,0:T(8,128)(2,1)} %get-tuple-element.113.embed_hbm, ...), custom_call_target="tpu_custom_call" | custom-call | tf_op jit(solution)/shard_map/cond/branch_1_fun/pallas_call | solution.py:488
  77.8 0.7 copy.43

commit v8 on v7

--- a/solution.py
+++ b/solution.py
@@ -12,7 +12,7 @@
 KEEP = 32
 HALF = KEEP // 2
 GROUP = 7
-SEMS = 16
+SEMS = 15
 REACH = 2
 OWN = 16
 NEAR_ROWS = 256
@@ -210,7 +210,7 @@
     def wait_out(ref, k):
         to_graph(ref, ref, k, me).wait_send()
 
-    DST, EMB, BASE, NEAR, PART, FWDB, FWDN, HID, PRJ, BACK, NBACK, HOT, PRJ0, BACK1, HIDH, PRJH = range(SEMS)
+    DST, EMB, BASE, NEAR, PART, FWDB, FWDN, HID, PRJ, BACK, NBACK, HOT, PRJ0, HIDH, PRJH = range(SEMS)
 
     blocks = (n * HALF) // CHUNK
     capacity = dst_ref.shape[2]
@@ -274,7 +274,7 @@
     WDEC.wait()
     w_other = wdec_ref[:, pl.ds(pl.multiple_of(other * quarter, quarter), quarter)]
     w_own = wdec_ref[:, pl.ds(pl.multiple_of(core * quarter, quarter), quarter)]
-    prj_out[...] = dot(embed_ref[...], w_other)
+    prj_out[...] = dot(embed_ref[...], w_other).astype(bf)
     send0 = to_core(prj_out, emb_half, PRJ0)
     send0.start()
     WSRC.wait()
@@ -283,7 +283,7 @@
     msgs = silu(dot(pick_turned(grid_ref[...], hot_src).T.astype(bf), wsrc_ref[...]) + bias_ref[...]).astype(bf)
     emb_own = dot(embed_ref[...], w_own)
     send0.wait_recv()
-    emb_out[...] = (emb_own + emb_half[...]).astype(bf).reshape(owners, OWN, quarter)
+    emb_out[...] = (emb_own + emb_half[...].astype(jnp.float32)).astype(bf).reshape(owners, OWN, quarter)
 
     wait_in(dst_in.at[pl.ds(0, n - 1)], DST)
     hot_dst = jnp.where(hot_src >= 0, dst_in[hot], -1)
@@ -324,20 +324,27 @@
     n_other = wnode_ref[:, pl.ds(pl.multiple_of(other * half, half), half)]
     n_own = wnode_ref[:, pl.ds(pl.multiple_of(core * half, half), half)]
     agg = (acc[...] + half_sum(other)).astype(bf)
-    hid_out[...] = dot(agg, n_other)
+    hid_out[...] = dot(agg, n_other).astype(bf)
     send = to_core(hid_out, hid_in, HID)
     send.start()
     own = dot(agg, n_own)
     send0.wait_send()
     send.wait_recv()
-    lat = (embed_ref[...].astype(jnp.float32) + silu(own + hid_in[...])).astype(bf)
-    prj_out[...] = dot(lat, w_other)
+    lat = (embed_ref[...].astype(jnp.float32) + silu(own + hid_in[...].astype(jnp.float32))).astype(bf)
+    prj_out[...] = dot(lat, w_other).astype(bf)
     send2 = to_core(prj_out, prj_in, PRJ)
     send2.start()
     own_p = dot(lat, w_own)
 
     send2.wait_recv()
-    prj_bf[...] = (own_p + prj_in[...]).astype(bf)
+    prj_bf[...] = (own_p + prj_in[...].astype(jnp.float32)).astype(bf)
+    for h in range(2):
+        for j in range(blocks):
+            rows = pick_turned(prj_bf[...], dstx_ref[h, j:j + 1]).T.astype(bf)
+            back_out[h, j * (CHUNK // HALF):(j + 1) * (CHUNK // HALF)] = rows.reshape(CHUNK // HALF, HALF, quarter)
+        back_in[h, pl.ds(me, 1)] = back_out[h, pl.ds(me, 1)]
+
+    each_peer(lambda peer: to_graph(back_out.at[:, peer], back_in.at[:, me], BACK, peer).start())
     for h in range(2):
         nback_out[h] = pick_turned(prj_bf[...], dstx_ref[h, blocks:]).T.astype(bf)
         nback_in[h, used:, :] = jnp.zeros((NEAR_ROWS - used, quarter), bf)
@@ -348,13 +355,6 @@
             else:
                 to_graph(nback_out.at[h, pl.ds(a, span)], nback_in.at[h, pl.ds(a, span)], NBACK, lax.rem(me - o + n, n)).start()
 
-    for h in range(2):
-        for j in range(blocks):
-            rows = pick_turned(prj_bf[...], dstx_ref[h, j:j + 1]).T.astype(bf)
-            back_out[h, j * (CHUNK // HALF):(j + 1) * (CHUNK // HALF)] = rows.reshape(CHUNK // HALF, HALF, quarter)
-        back_in[h, pl.ds(me, 1)] = back_out[h, pl.ds(me, 1)]
-        each_peer(lambda peer, h=h: to_graph(back_out.at[h, peer], back_in.at[h, me], BACK1 if h else BACK, peer).start())
-
     @pl.when(mine)
     def _():
         wait_in(part_in.at[pl.ds(0, n - 1)], PART)
@@ -390,13 +390,13 @@
     for h in range(2):
         total = total + dot(spread(grid_rows, srcx_ref[h, blocks:]), nback_in[h])
     dec[...] = total
+    wait_in(back_in.at[:, pl.ds(0, n - 1)], BACK)
+    total = dec[...]
     for h in range(2):
-        wait_in(back_in.at[h, pl.ds(0, n - 1)], BACK1 if h else BACK)
-        total = dec[...]
         for j in range(blocks):
             rows = back_in[h, j * (CHUNK // HALF):(j + 1) * (CHUNK // HALF)].reshape(CHUNK, quarter)
             total = total + dot(spread(grid_rows, srcx_ref[h, j:j + 1]), rows)
-        dec[...] = total
+    dec[...] = total
 
     @pl.when(mine)
     def _():
@@ -430,8 +430,7 @@
     to_core(near_in.at[core], near_in.at[core], FWDN).wait_send()
     for copy in (send, send2, send3, send4):
         copy.wait_send()
-    for h in range(2):
-        wait_out(back_out.at[h, pl.ds(0, n - 1)], BACK1 if h else BACK)
+    wait_out(back_out.at[:, pl.ds(0, n - 1)], BACK)
     wait_out(nback_out.at[:, pl.ds(0, 2 * REACH * span)], NBACK)
 
 
@@ -497,11 +496,11 @@
             vm((2, n * HALF // CHUNK + 1, CHUNK), jnp.int32), vm((2, n * HALF // CHUNK + 1, CHUNK), jnp.int32),
             vm((n, HALF, width), bf), vm((NEAR_ROWS, width), bf),
             vm((2, n, HALF, width), bf), vm((2, NEAR_ROWS, width), bf),
-            vm((n, 1, capacity), jnp.int32), vm((n, OWN, quarter), bf), vm((owners, OWN, quarter), bf), vm((mesh_rows, quarter), f32),
+            vm((n, 1, capacity), jnp.int32), vm((n, OWN, quarter), bf), vm((owners, OWN, quarter), bf), vm((mesh_rows, quarter), bf),
             vm((owners, OWN, half), bf), vm((n, OWN, half), bf),
             vm((mesh_rows, half), f32),
-            vm((mesh_rows, half), f32), vm((mesh_rows, half), f32),
-            vm((mesh_rows, quarter), f32), vm((mesh_rows, quarter), f32), vm((mesh_rows, quarter), bf),
+            vm((mesh_rows, half), bf), vm((mesh_rows, half), bf),
+            vm((mesh_rows, quarter), bf), vm((mesh_rows, quarter), bf), vm((mesh_rows, quarter), bf),
             vm((2, n, HALF, quarter), bf), vm((2, NEAR_ROWS, quarter), bf),
             vm((2, n, HALF, quarter), bf), vm((2, NEAR_ROWS, quarter), bf),
             vm((OWN, quarter), bf), vm((owners, OWN, quarter), bf),

time: 78.7 us -> 78.1 us (level)
  the two profiles are of different devices: /device:TPU:513 before, /device:TPU:640 now
where the time goes in v8:
time: 78.1 us; the launch traced here: 76.8 us
  Pallas kernels  73.2 us (94%)
  other arithmetic  1.49 us (2%)
  between operations  1.3 us (2%)
    pallas_call x1, Pallas kernels, compact(): pl.pallas_call(functools.partial(step_kernel, n), out_shape=jax.ShapeDtyp...  73.2 us

profile of v8, /device:TPU:640, one launch (start us, length us, event | category | flops | bytes accessed | tf_op | source)
XLA Modules:
  0.0 76.8 jit_solution(6356106884254451284)
XLA Ops:
  0.0 1.5 %select_reduce_fusion = (s32[]{:T(128)}, s32[]{:T(128)}) fusion(s32[64,64]{1,0:T(8,128)} %param.23), kind=kLoop, calls=%fused_computation.52 | loop fusion | flops 45054 | bytes 16392 | tf_op jit(solution)/shard_map/reduce_min | solution.py:523
  2.8 73.4 %conditional.1 = (bf16[1024,128]{1,0:T(8,128)(2,1)S(1)}) conditional(s32[]{:T(128)} %convert_element_type.26, (bf16[1024,256]{1,0:T(8,128)(2,1)}, s32[64,64]{1,0:T(8,128)}, s32[1,64,128]{2,1,0:T(8,128)}, s32[64,1,128]{2,1,0:T(1,128)}, bf16[640,256]{1,0:T(8,128)(2,1)}, /*index=5*/bf16[256,256]{1,0:T(8,128)(2,1)}, f32[256]{0:T(256)}, ...), branch_computations={%region_2.9_spmd, %region_9.10_spmd} | conditional | flops 2573017088 | bytes 80659304 | solution.py:526
  3.0 73.2 %branch_1_fun.1 = bf16[1024,128]{1,0:T(8,128)(2,1)S(1)} custom-call(s32[1]{0:T(128)} %bitcast.17.hot_ref, bf16[1024,256]{1,0:T(8,128)(2,1)} %get-tuple-element.110.grid_hbm, bf16[256,256]{1,0:T(8,128)(2,1)} %get-tuple-element.111.wsrc_hbm, f32[1,256]{1,0:T(1,128)} %bitcast.72, bf16[640,256]{1,0:T(8,128)(2,1)} %get-tuple-element.113.embed_hbm, ...), custom_call_target="tpu_custom_call" | custom-call | tf_op jit(solution)/shard_map/cond/branch_1_fun/pallas_call | solution.py:487
  76.1 0.7 copy.43

commit v9 on v8

--- a/solution.py
+++ b/solution.py
@@ -134,12 +134,12 @@
 
 
 def step_kernel(
-    n, hot_ref, grid_hbm, wsrc_hbm, bias_hbm, embed_hbm, wnode_hbm, wdec_hbm, src_hbm, dst_hbm, count_hbm, out_ref,
+    n, grid_hbm, wsrc_hbm, bias_hbm, embed_hbm, wnode_hbm, wdec_hbm, src_hbm, dst_hbm, count_hbm, out_ref, fits_ref,
     grid_ref, wsrc_ref, bias_ref, embed_ref, wnode_ref, wdec_ref, src_ref, dst_ref, count_ref,
     src_live, dst_live, srcx_ref, dstx_ref,
     base_out, near_out, base_in, near_in, dst_in, emb_in, emb_out, emb_half, part_out, part_in,
     acc, hid_out, hid_in, prj_out, prj_in, prj_bf, back_out, nback_out, back_in, nback_in, hot_out, hot_in, dec,
-    hhid_out, hhid_in, hprj_out, hprj_in,
+    hhid_out, hhid_in, hprj_out, hprj_in, hot_to, hot_from,
     lsem, ssem, rsem,
 ):
     me = lax.axis_index("graph")
@@ -218,10 +218,14 @@
     DSTS.wait()
     COUNT.wait()
     with jax.named_scope("index"):
-        hot = hot_ref[0]
         ids = lax.broadcasted_iota(jnp.int32, (n, n), 0)
         cols = lax.broadcasted_iota(jnp.int32, (n, n), 1)
         counts = count_ref[...]
+        apart = jnp.abs(ids - cols)
+        far_counts = jnp.where(jnp.minimum(apart, n - apart) > REACH, counts, 0)
+        hot = jnp.max(jnp.where(far_counts > KEEP, cols, 0))
+        first = jnp.min(jnp.where(far_counts > KEEP, cols, n))
+        fits_ref[0] = jnp.where(hot <= first, 1, 0)
         sent = jnp.where(ids == me, counts, 0).sum(axis=0, keepdims=True)
         sent = jnp.where(ids == cols, sent, 0).sum(axis=1, keepdims=True)
         came = jnp.where(cols == me, counts, 0).sum(axis=1, keepdims=True)
@@ -398,6 +402,9 @@
             total = total + dot(spread(grid_rows, srcx_ref[h, j:j + 1]), rows)
     dec[...] = total
 
+    hot_to[...] = spread(grid_rows, hot_src)
+    hot_from[...] = spread(mesh_rows, hot_dst)
+
     @pl.when(mine)
     def _():
         wait_in(hot_in.at[pl.ds(0, owners - 1)], HOT)
@@ -407,8 +414,10 @@
     def _():
         wait_in(hot_in, HOT)
 
-    hot_rows = pick_turned(hot_in[...].reshape(mesh_rows, quarter), hot_dst).astype(bf)
-    back = lax.dot_general(spread(grid_rows, hot_src), hot_rows, (((1,), (1,)), ((), ())), preferred_element_type=jnp.float32)
+    hot_rows = lax.dot_general(
+        hot_in[...].reshape(mesh_rows, quarter), hot_from[...], (((0,), (0,)), ((), ())), preferred_element_type=jnp.float32
+    ).astype(bf)
+    back = lax.dot_general(hot_to[...], hot_rows, (((1,), (1,)), ((), ())), preferred_element_type=jnp.float32)
     out_ref[...] = (dec[...] + back).astype(bf)
 
     wait_out(dst_ref.at[pl.ds(0, n - 1)], DST)
@@ -475,7 +484,7 @@
     return take, inside * jnp.where(row < count, 1.0, 0.0)
 
 
-def compact(hot, grid_state, w_src, bias_src, mesh_embed, w_node, w_dec, slot_src, slot_dst, slot_count):
+def compact(grid_state, w_src, bias_src, mesh_embed, w_node, w_dec, slot_src, slot_dst, slot_count):
     n = lax.axis_size("graph")
     capacity = slot_src.shape[2]
     grid_rows, width = grid_state.shape
@@ -486,9 +495,9 @@
     vm = pltpu.VMEM
     return pl.pallas_call(
         functools.partial(step_kernel, n),
-        out_shape=jax.ShapeDtypeStruct((grid_rows, quarter), bf),
-        in_specs=[pl.BlockSpec(memory_space=pltpu.SMEM)] + [pl.BlockSpec(memory_space=pl.ANY)] * 9,
-        out_specs=pl.BlockSpec(memory_space=vm),
+        out_shape=(jax.ShapeDtypeStruct((grid_rows, quarter), bf), jax.ShapeDtypeStruct((1,), jnp.int32)),
+        in_specs=[pl.BlockSpec(memory_space=pl.ANY)] * 9,
+        out_specs=(pl.BlockSpec(memory_space=vm), pl.BlockSpec(memory_space=pltpu.SMEM)),
         scratch_shapes=[
             vm((grid_rows, width), bf), vm(w_src.shape, bf), vm((1, half), f32), vm((mesh_rows, half), bf), vm(w_node.shape, bf),
             vm(w_dec.shape, bf), vm(slot_src.shape, jnp.int32), vm(slot_dst.shape, jnp.int32), vm(slot_count.shape, jnp.int32),
@@ -506,24 +515,17 @@
             vm((OWN, quarter), bf), vm((owners, OWN, quarter), bf),
             vm((grid_rows, quarter), f32),
             vm((OWN, half), f32), vm((OWN, half), f32), vm((OWN, quarter), f32), vm((OWN, quarter), f32),
+            vm((grid_rows, capacity), bf), vm((mesh_rows, capacity), bf),
             pltpu.SemaphoreType.DMA((9,)), pltpu.SemaphoreType.DMA((SEMS,)), pltpu.SemaphoreType.DMA((SEMS,)),
         ],
         compiler_params=pltpu.CompilerParams(collective_id=0, has_side_effects=True, vmem_limit_bytes=48 * 1024 * 1024),
-    )(hot, grid_state, w_src, bias_src[None, :], mesh_embed, w_node, w_dec, slot_src, slot_dst, slot_count)
+    )(grid_state, w_src, bias_src[None, :], mesh_embed, w_node, w_dec, slot_src, slot_dst, slot_count)
 
 
 def on_device(grid_state, w_src, bias_src, mesh_embed, w_node, w_dec, slot_src, slot_dst, slot_count):
     args = (grid_state, w_src, bias_src, mesh_embed, w_node, w_dec, slot_src, slot_dst, slot_count)
-    n = slot_count.shape[0]
-    apart = jnp.abs(jnp.arange(n)[:, None] - jnp.arange(n)[None, :])
-    far = jnp.minimum(apart, n - apart) > REACH
-    over = far & (slot_count > KEEP)
-    column = jnp.broadcast_to(jnp.arange(n, dtype=jnp.int32)[None, :], (n, n))
-    last = jnp.max(jnp.where(over, column, 0))
-    first = jnp.min(jnp.where(over, column, n))
-    fits = last <= first
-    hot = last.reshape(1)
-    return lax.cond(fits, lambda: compact(hot, *args), lambda: dense(*args))
+    result, fits = compact(*args)
+    return lax.cond(fits[0] > 0, lambda: result, lambda: dense(*args))
 
 
 def solution(mesh):

time: 78.1 us -> 75.8 us (0.971)
  other arithmetic: 1.49 us -> 0 us
    reduce_min x1 -> x0, other arithmetic: 1.49 us -> none  [on_device(): first = jnp.min(jnp.where(over, column, n))]
where the time goes in v9:
time: 75.8 us; the launch traced here: 74.6 us
  Pallas kernels  73 us (96%)
    pallas_call x1, Pallas kernels, compact(): pl.pallas_call(functools.partial(step_kernel, n), out_shape=(jax.ShapeDty...  73 us

profile of v9, /device:TPU:640, one launch (start us, length us, event | category | flops | bytes accessed | tf_op | source)
XLA Modules:
  0.0 74.6 jit_solution(11675060152837438313)
XLA Ops:
  0.0 73.0 %shard_map.93 = (bf16[1024,128]{1,0:T(8,128)(2,1)S(1)}, s32[1]{0:T(128)}) custom-call(bf16[1024,256]{1,0:T(8,128)(2,1)} %grid_hbm.1, bf16[256,256]{1,0:T(8,128)(2,1)} %wsrc_hbm.1, f32[1,256]{1,0:T(1,128)} %bitcast.72, bf16[640,256]{1,0:T(8,128)(2,1)} %embed_hbm.1, bf16[256,512]{1,0:T(8,128)(2,1)} %wnode_hbm.1, bf16[256,256]{1,0:T(8,128)(2,1)} %wdec_hbm.1, ...), custom_call_target="tpu_custom_call" | custom-call | tf_op jit(solution)/shard_map/pallas_call | solution.py:496
  73.7 0.2 conditional.1
  73.9 0.7 copy.43

commit v10 on v9

--- a/solution.py
+++ b/solution.py
@@ -12,7 +12,7 @@
 KEEP = 32
 HALF = KEEP // 2
 GROUP = 7
-SEMS = 15
+SEMS = 17
 REACH = 2
 OWN = 16
 NEAR_ROWS = 256
@@ -210,7 +210,7 @@
     def wait_out(ref, k):
         to_graph(ref, ref, k, me).wait_send()
 
-    DST, EMB, BASE, NEAR, PART, FWDB, FWDN, HID, PRJ, BACK, NBACK, HOT, PRJ0, HIDH, PRJH = range(SEMS)
+    DST, EMB, BASE, NEAR, PART, FWDB, FWDN, HID, PRJ, BACK, NBACK, HOT, PRJ0, HIDH, PRJH, HID1, PRJ1 = range(SEMS)
 
     blocks = (n * HALF) // CHUNK
     capacity = dst_ref.shape[2]
@@ -303,12 +303,13 @@
         return visit
 
     each_peer(to_owner(lambda peer, block: to_graph(part_out.at[block], part_in.at[me], PART, peer)))
-    each_peer(to_owner(lambda peer, block: to_graph(emb_out.at[block], emb_in.at[me], EMB, peer)))
 
     wait_in(base_in.at[core, pl.ds(0, n - 1)], BASE)
     to_core(base_in.at[core], base_in.at[core], FWDB).start()
     wait_in(near_in.at[core, pl.ds(0, 2 * REACH * span)], NEAR)
     to_core(near_in.at[core], near_in.at[core], FWDN).start()
+    each_peer(to_owner(lambda peer, block: to_graph(emb_out.at[block], emb_in.at[me], EMB, peer)))
+
     def share(rows, idx):
         m = silu(dot(rows, wsrc_ref[...]) + bias_ref[...]).astype(bf)
         return dot(spread(mesh_rows, idx), m)
@@ -328,20 +329,26 @@
     n_other = wnode_ref[:, pl.ds(pl.multiple_of(other * half, half), half)]
     n_own = wnode_ref[:, pl.ds(pl.multiple_of(core * half, half), half)]
     agg = (acc[...] + half_sum(other)).astype(bf)
-    hid_out[...] = dot(agg, n_other).astype(bf)
-    send = to_core(hid_out, hid_in, HID)
-    send.start()
-    own = dot(agg, n_own)
+    middle = mesh_rows // 2
+    spans = (slice(0, middle), slice(middle, mesh_rows))
+    sends, own, own_p = [], [], []
+    for part, k in zip(spans, (HID, HID1)):
+        hid_out[part] = dot(agg[part], n_other).astype(bf)
+        sends.append(to_core(hid_out.at[part], hid_in.at[part], k))
+        sends[-1].start()
+    for part in spans:
+        own.append(dot(agg[part], n_own))
     send0.wait_send()
-    send.wait_recv()
-    lat = (embed_ref[...].astype(jnp.float32) + silu(own + hid_in[...].astype(jnp.float32))).astype(bf)
-    prj_out[...] = dot(lat, w_other).astype(bf)
-    send2 = to_core(prj_out, prj_in, PRJ)
-    send2.start()
-    own_p = dot(lat, w_own)
-
-    send2.wait_recv()
-    prj_bf[...] = (own_p + prj_in[...].astype(jnp.float32)).astype(bf)
+    for i, (part, k) in enumerate(zip(spans, (PRJ, PRJ1))):
+        sends[i].wait_recv()
+        lat = (embed_ref[part].astype(jnp.float32) + silu(own[i] + hid_in[part].astype(jnp.float32))).astype(bf)
+        prj_out[part] = dot(lat, w_other).astype(bf)
+        sends.append(to_core(prj_out.at[part], prj_in.at[part], k))
+        sends[-1].start()
+        own_p.append(dot(lat, w_own))
+    for i, part in enumerate(spans):
+        sends[2 + i].wait_recv()
+        prj_bf[part] = (own_p[i] + prj_in[part].astype(jnp.float32)).astype(bf)
     for h in range(2):
         for j in range(blocks):
             rows = pick_turned(prj_bf[...], dstx_ref[h, j:j + 1]).T.astype(bf)
@@ -349,6 +356,36 @@
         back_in[h, pl.ds(me, 1)] = back_out[h, pl.ds(me, 1)]
 
     each_peer(lambda peer: to_graph(back_out.at[:, peer], back_in.at[:, me], BACK, peer).start())
+    @pl.when(mine)
+    def _():
+        wait_in(part_in.at[pl.ds(0, n - 1)], PART)
+        part_in[pl.ds(me, 1)] = part_out[pl.ds(my_block, 1)]
+
+    hot_agg = part_in[...].astype(jnp.float32).sum(axis=0).astype(bf)
+    hhid_out[...] = dot(hot_agg, n_other)
+    send3 = to_core(hhid_out, hhid_in, HIDH)
+    send3.start()
+    hot_own = dot(hot_agg, n_own)
+
+    send3.wait_recv()
+    hot_lat = silu(hot_own + hhid_in[...]).astype(bf)
+    hprj_out[...] = dot(hot_lat, w_other)
+    send4 = to_core(hprj_out, hprj_in, PRJH)
+    send4.start()
+    hot_prj = dot(hot_lat, w_own)
+
+    @pl.when(mine)
+    def _():
+        wait_in(emb_in.at[pl.ds(0, n - 1)], EMB)
+        emb_in[pl.ds(me, 1)] = emb_out[pl.ds(my_block, 1)]
+
+    send4.wait_recv()
+    hot_out[...] = (hot_prj + hprj_in[...] + emb_in[hot].astype(jnp.float32)).astype(bf)
+
+    @pl.when(mine)
+    def _():
+        each_peer(lambda peer: to_graph(hot_out, hot_in.at[my_block], HOT, peer).start())
+
     for h in range(2):
         nback_out[h] = pick_turned(prj_bf[...], dstx_ref[h, blocks:]).T.astype(bf)
         nback_in[h, used:, :] = jnp.zeros((NEAR_ROWS - used, quarter), bf)
@@ -358,36 +395,6 @@
                 nback_in[h, a:a + span] = nback_out[h, a:a + span]
             else:
                 to_graph(nback_out.at[h, pl.ds(a, span)], nback_in.at[h, pl.ds(a, span)], NBACK, lax.rem(me - o + n, n)).start()
-
-    @pl.when(mine)
-    def _():
-        wait_in(part_in.at[pl.ds(0, n - 1)], PART)
-        part_in[pl.ds(me, 1)] = part_out[pl.ds(my_block, 1)]
-
-    hot_agg = part_in[...].astype(jnp.float32).sum(axis=0).astype(bf)
-    hhid_out[...] = dot(hot_agg, n_other)
-    send3 = to_core(hhid_out, hhid_in, HIDH)
-    send3.start()
-    hot_own = dot(hot_agg, n_own)
-
-    send3.wait_recv()
-    hot_lat = silu(hot_own + hhid_in[...]).astype(bf)
-    hprj_out[...] = dot(hot_lat, w_other)
-    send4 = to_core(hprj_out, hprj_in, PRJH)
-    send4.start()
-    hot_prj = dot(hot_lat, w_own)
-
-    @pl.when(mine)
-    def _():
-        wait_in(emb_in.at[pl.ds(0, n - 1)], EMB)
-        emb_in[pl.ds(me, 1)] = emb_out[pl.ds(my_block, 1)]
-
-    send4.wait_recv()
-    hot_out[...] = (hot_prj + hprj_in[...] + emb_in[hot].astype(jnp.float32)).astype(bf)
-
-    @pl.when(mine)
-    def _():
-        each_peer(lambda peer: to_graph(hot_out, hot_in.at[my_block], HOT, peer).start())
 
     wait_in(nback_in.at[:, pl.ds(0, 2 * REACH * span)], NBACK)
     total = grid_ref[:, pl.ds(pl.multiple_of(core * quarter, quarter), quarter)].astype(jnp.float32)
@@ -437,7 +444,7 @@
 
     to_core(base_in.at[core], base_in.at[core], FWDB).wait_send()
     to_core(near_in.at[core], near_in.at[core], FWDN).wait_send()
-    for copy in (send, send2, send3, send4):
+    for copy in (*sends, send3, send4):
         copy.wait_send()
     wait_out(back_out.at[:, pl.ds(0, n - 1)], BACK)
     wait_out(nback_out.at[:, pl.ds(0, 2 * REACH * span)], NBACK)

time: 75.8 us -> 76.1 us (level); the launches traced: 74.6 us -> 75.7 us
  Pallas kernels: 73 us -> 74.1 us
    pallas_call x1, Pallas kernels: 73 us -> 74.1 us  [compact(): pl.pallas_call(functools.partial(step_kernel, n), out_shape=(jax.ShapeDty...]
where the time goes in v10:
time: 76.1 us; the launch traced here: 75.7 us
  Pallas kernels  74.1 us (97%)
    pallas_call x1, Pallas kernels, compact(): pl.pallas_call(functools.partial(step_kernel, n), out_shape=(jax.ShapeDty...  74.1 us

profile of v10, /device:TPU:640, one launch (start us, length us, event | category | flops | bytes accessed | tf_op | source)
XLA Modules:
  0.0 75.7 jit_solution(7335706549087745151)
XLA Ops:
  0.0 74.1 %shard_map.93 = (bf16[1024,128]{1,0:T(8,128)(2,1)S(1)}, s32[1]{0:T(128)}) custom-call(bf16[1024,256]{1,0:T(8,128)(2,1)} %grid_hbm.1, bf16[256,256]{1,0:T(8,128)(2,1)} %wsrc_hbm.1, f32[1,256]{1,0:T(1,128)} %bitcast.72, bf16[640,256]{1,0:T(8,128)(2,1)} %embed_hbm.1, bf16[256,512]{1,0:T(8,128)(2,1)} %wnode_hbm.1, bf16[256,256]{1,0:T(8,128)(2,1)} %wdec_hbm.1, ...), custom_call_target="tpu_custom_call" | custom-call | tf_op jit(solution)/shard_map/pallas_call | solution.py:503
  74.8 0.2 conditional.1
  75.0 0.7 copy.43

commit v11 on v10

--- a/solution.py
+++ b/solution.py
@@ -303,13 +303,12 @@
         return visit
 
     each_peer(to_owner(lambda peer, block: to_graph(part_out.at[block], part_in.at[me], PART, peer)))
+    each_peer(to_owner(lambda peer, block: to_graph(emb_out.at[block], emb_in.at[me], EMB, peer)))
 
     wait_in(base_in.at[core, pl.ds(0, n - 1)], BASE)
     to_core(base_in.at[core], base_in.at[core], FWDB).start()
     wait_in(near_in.at[core, pl.ds(0, 2 * REACH * span)], NEAR)
     to_core(near_in.at[core], near_in.at[core], FWDN).start()
-    each_peer(to_owner(lambda peer, block: to_graph(emb_out.at[block], emb_in.at[me], EMB, peer)))
-
     def share(rows, idx):
         m = silu(dot(rows, wsrc_ref[...]) + bias_ref[...]).astype(bf)
         return dot(spread(mesh_rows, idx), m)

time: 76.1 us -> 79.1 us (1.039)
  Pallas kernels: 74.1 us -> 77.4 us
    pallas_call x1, Pallas kernels: 74.1 us -> 77.4 us  [compact(): pl.pallas_call(functools.partial(step_kernel, n), out_shape=(jax.ShapeDty...]
where the time goes in v11:
time: 79.1 us; the launch traced here: 79 us
  Pallas kernels  77.4 us (98%)
    pallas_call x1, Pallas kernels, compact(): pl.pallas_call(functools.partial(step_kernel, n), out_shape=(jax.ShapeDty...  77.4 us

profile of v11, /device:TPU:640, one launch (start us, length us, event | category | flops | bytes accessed | tf_op | source)
XLA Modules:
  0.0 79.0 jit_solution(8458363364647474719)
XLA Ops:
  0.0 77.4 %shard_map.93 = (bf16[1024,128]{1,0:T(8,128)(2,1)S(1)}, s32[1]{0:T(128)}) custom-call(bf16[1024,256]{1,0:T(8,128)(2,1)} %grid_hbm.1, bf16[256,256]{1,0:T(8,128)(2,1)} %wsrc_hbm.1, f32[1,256]{1,0:T(1,128)} %bitcast.72, bf16[640,256]{1,0:T(8,128)(2,1)} %embed_hbm.1, bf16[256,512]{1,0:T(8,128)(2,1)} %wnode_hbm.1, bf16[256,256]{1,0:T(8,128)(2,1)} %wdec_hbm.1, ...), custom_call_target="tpu_custom_call" | custom-call | tf_op jit(solution)/shard_map/pallas_call | solution.py:502
  78.0 0.2 conditional.1
  78.3 0.7 copy.43

commit v12 on v9

--- a/solution.py
+++ b/solution.py
@@ -303,12 +303,13 @@
         return visit
 
     each_peer(to_owner(lambda peer, block: to_graph(part_out.at[block], part_in.at[me], PART, peer)))
-    each_peer(to_owner(lambda peer, block: to_graph(emb_out.at[block], emb_in.at[me], EMB, peer)))
 
     wait_in(base_in.at[core, pl.ds(0, n - 1)], BASE)
     to_core(base_in.at[core], base_in.at[core], FWDB).start()
     wait_in(near_in.at[core, pl.ds(0, 2 * REACH * span)], NEAR)
     to_core(near_in.at[core], near_in.at[core], FWDN).start()
+    each_peer(to_owner(lambda peer, block: to_graph(emb_out.at[block], emb_in.at[me], EMB, peer)))
+
     def share(rows, idx):
         m = silu(dot(rows, wsrc_ref[...]) + bias_ref[...]).astype(bf)
         return dot(spread(mesh_rows, idx), m)

time: 75.8 us -> 75.2 us (level)
  no operation moved by 1% of the time
where the time goes in v12:
time: 75.2 us; the launch traced here: 74.2 us
  Pallas kernels  72.7 us (97%)
    pallas_call x1, Pallas kernels, compact(): pl.pallas_call(functools.partial(step_kernel, n), out_shape=(jax.ShapeDty...  72.7 us

profile of v12, /device:TPU:640, one launch (start us, length us, event | category | flops | bytes accessed | tf_op | source)
XLA Modules:
  0.0 74.2 jit_solution(884819408231275118)
XLA Ops:
  0.0 72.7 %shard_map.93 = (bf16[1024,128]{1,0:T(8,128)(2,1)S(1)}, s32[1]{0:T(128)}) custom-call(bf16[1024,256]{1,0:T(8,128)(2,1)} %grid_hbm.1, bf16[256,256]{1,0:T(8,128)(2,1)} %wsrc_hbm.1, f32[1,256]{1,0:T(1,128)} %bitcast.72, bf16[640,256]{1,0:T(8,128)(2,1)} %embed_hbm.1, bf16[256,512]{1,0:T(8,128)(2,1)} %wnode_hbm.1, bf16[256,256]{1,0:T(8,128)(2,1)} %wdec_hbm.1, ...), custom_call_target="tpu_custom_call" | custom-call | tf_op jit(solution)/shard_map/pallas_call | solution.py:497
  73.3 0.2 conditional.1
  73.5 0.7 copy.43
